TPU v7x, 32 devices: a whole 2x2x4 slice. The times are simulated.
32 devices in a mesh: pair: 2 (over x), tp: 4 (over z), side: 4 (over y, core).
Axes of the slice: x: 2, y: 2, z: 4, core: 2. Of those that a mesh axis runs over, the one named last changes fastest.
Arguments:
- prompt_x: bfloat16 [8192, 2048], P(('pair', 'side')), parts along dimension 0
- s_len: int32 [8], P(('pair', 'side')), parts along dimension 0
- w_qkv_pre: bfloat16 [2, 2048, 3, 16, 128], P(None, None, None, 'tp')
- w_out_pre: bfloat16 [2, 16, 128, 2048], P(None, 'tp')
- w_gu_pre: bfloat16 [2, 2, 5504, 2048], P(None, None, 'tp')
- w_down_pre: bfloat16 [2, 5504, 2048], P(None, 'tp')
- gain_pre: float32 [2, 2, 2048], replicated
- dec_tokens: bfloat16 [64, 2048], P(('pair', 'side')), parts along dimension 0
- k_cache: bfloat16 [2, 64, 256, 4, 4, 128], P(None, ('pair', 'side'), None, None, 'tp'), parts along dimension 1
- v_cache: bfloat16 [2, 64, 256, 4, 4, 128], P(None, ('pair', 'side'), None, None, 'tp'), parts along dimension 1
- c_len: int32 [64], P(('pair', 'side')), parts along dimension 0
- w_qkv_dec: bfloat16 [2, 2048, 3, 4, 4, 128], P(None, None, None, None, 'tp')
- w_out_dec: bfloat16 [2, 4, 4, 128, 2048], P(None, None, 'tp')
- w_gu_dec: bfloat16 [2, 2, 5504, 2048], P(None, None, 'tp')
- w_down_dec: bfloat16 [2, 5504, 2048], P(None, 'tp')
- gain_dec: float32 [2, 2, 2048], replicated
Outputs:
- output 1: bfloat16 [8192, 2048], P(('pair', 'side')), parts along dimension 0
- output 2: bfloat16 [64, 2048], P(('pair', 'side')), parts along dimension 0
- output 3: bfloat16 [2, 8192, 4, 4, 128], P(None, ('pair', 'side'), None, 'tp'), parts along dimension 1
- output 4: bfloat16 [2, 8192, 4, 4, 128], P(None, ('pair', 'side'), None, 'tp'), parts along dimension 1
- output 5: bfloat16 [2, 64, 256, 4, 4, 128], P(None, ('pair', 'side'), None, None, 'tp'), parts along dimension 1
- output 6: bfloat16 [2, 64, 256, 4, 4, 128], P(None, ('pair', 'side'), None, None, 'tp'), parts along dimension 1
There are 2 independent parts. A program takes and returns all parts, laid end to end along the dimension named above; an argument that names none is the same for every part.
All inputs are finite; a program needn't handle non-finite values.
Results may differ from a plain program's by a relative error of at most 0.02.
Values are sent between devices in bfloat16 or wider.
A program may use at most 1 GiB of HBM per device.

v0:
```python
import jax
import jax.numpy as jnp
from jax import lax
from jax.sharding import PartitionSpec as P

EPSILON = 1e-6
THETA = 10000.0
MASKED = -1e30


def rms_norm(hidden, gain_vec):
    hid_f32 = hidden.astype(jnp.float32)
    inv_rms = lax.rsqrt(jnp.mean(hid_f32 * hid_f32, axis=-1, keepdims=True) + EPSILON)
    return (hid_f32 * inv_rms * gain_vec).astype(jnp.bfloat16)


def add_residual(hidden, update):
    return (hidden.astype(jnp.float32) + update.astype(jnp.float32)).astype(jnp.bfloat16)


def rope_tables(positions, head_dim):
    half_dim = head_dim // 2
    inv_freq = THETA ** (-jnp.arange(half_dim, dtype=jnp.float32) * 2.0 / head_dim)
    angles = positions.astype(jnp.float32)[:, None] * inv_freq[None, :]
    return jnp.cos(angles), jnp.sin(angles)


def apply_rope(values_in, cos_tab, sin_tab):
    half_dim = values_in.shape[-1] // 2
    lower_half = values_in[..., :half_dim]
    upper_half = values_in[..., half_dim:]
    cos_b = cos_tab[:, None, :]
    sin_b = sin_tab[:, None, :]
    return jnp.concatenate([lower_half * cos_b - upper_half * sin_b, upper_half * cos_b + lower_half * sin_b], axis=-1)


def swiglu(hidden, gain_vec, w_gu, w_down):
    normed = rms_norm(hidden, gain_vec)
    gate_up = jnp.einsum('...d,kfd->...kf', normed, w_gu, preferred_element_type=jnp.float32)
    gate_val = gate_up[..., 0, :].astype(jnp.bfloat16).astype(jnp.float32)
    up_val = gate_up[..., 1, :].astype(jnp.bfloat16).astype(jnp.float32)
    activated = (jax.nn.silu(gate_val) * up_val).astype(jnp.bfloat16)
    return jnp.einsum('...f,fd->...d', activated, w_down, preferred_element_type=jnp.float32)


def prompt_attention(queries, keys_in, values_in, allowed):
    attn_scale = queries.shape[-1] ** -0.5
    scores = jnp.einsum('nqhe,nkhe->nhqk', queries, keys_in, preferred_element_type=jnp.float32) * attn_scale
    scores = jnp.where(allowed[:, None], scores, MASKED)
    prob_bf = jax.nn.softmax(scores, axis=-1).astype(jnp.bfloat16)
    return jnp.einsum('nhqk,nkhe->nqhe', prob_bf, values_in, preferred_element_type=jnp.float32).astype(jnp.bfloat16)


def decode_attention(queries, k_tok, v_tok, k_layer, v_layer, visible):
    attn_scale = queries.shape[-1] ** -0.5
    cache_scores = jnp.einsum('bhe,bthe->bht', queries, k_layer, preferred_element_type=jnp.float32) * attn_scale
    cache_scores = jnp.where(visible, cache_scores, MASKED)
    self_score = jnp.einsum('bhe,bhe->bh', queries, k_tok, preferred_element_type=jnp.float32) * attn_scale
    row_max = jnp.maximum(jnp.max(cache_scores, axis=-1), self_score)
    cache_exp = jnp.exp(cache_scores - row_max[..., None])
    self_exp = jnp.exp(self_score - row_max)
    denominator = jnp.sum(cache_exp, axis=-1) + self_exp
    cache_prob = (cache_exp / denominator[..., None]).astype(jnp.bfloat16)
    self_prob = (self_exp / denominator).astype(jnp.bfloat16).astype(jnp.float32)
    context = jnp.einsum('bht,bthe->bhe', cache_prob, v_layer, preferred_element_type=jnp.float32) + self_prob[..., None] * v_tok.astype(jnp.float32)
    return context.astype(jnp.bfloat16)


def run_prefill(prompts, s_valid, w_qkv, w_out, w_gu, w_down, gains):
    seq_len = prompts.shape[1]
    positions = jnp.arange(seq_len)
    cos_tab, sin_tab = rope_tables(positions, w_qkv.shape[-1])
    allowed = (positions[None, :] <= positions[:, None])[None] & (positions[None, None, :] < s_valid[:, None, None])
    hidden = prompts
    kv_layers = []
    for layer_idx in range(w_qkv.shape[0]):
        normed = rms_norm(hidden, gains[layer_idx, 0])
        qkv_out = jnp.einsum('nsd,dkhe->nskhe', normed, w_qkv[layer_idx], preferred_element_type=jnp.float32)
        queries = apply_rope(qkv_out[:, :, 0], cos_tab, sin_tab).astype(jnp.bfloat16)
        keys_new = apply_rope(qkv_out[:, :, 1], cos_tab, sin_tab).astype(jnp.bfloat16)
        values_new = qkv_out[:, :, 2].astype(jnp.bfloat16)
        context = prompt_attention(queries, keys_new, values_new, allowed)
        part_sum = jnp.einsum('nshe,hed->nsd', context, w_out[layer_idx], preferred_element_type=jnp.float32)
        hidden = add_residual(hidden, lax.psum(part_sum, 'tp').astype(jnp.bfloat16))
        mlp_part = swiglu(hidden, gains[layer_idx, 1], w_gu[layer_idx], w_down[layer_idx])
        hidden = add_residual(hidden, lax.psum(mlp_part, 'tp').astype(jnp.bfloat16))
        kv_layers.append(jnp.stack([keys_new, values_new]))
    return hidden, kv_layers


def run_decode(tokens, k_cache, v_cache, c_len, w_qkv, w_out, w_gu, w_down, gains):
    layers = k_cache.shape[0]
    row_count = k_cache.shape[1]
    cache_len = k_cache.shape[2]
    heads_loc = k_cache.shape[3]
    head_dim = k_cache.shape[5]
    model_width = tokens.shape[1]
    k_local = k_cache.reshape(layers, row_count, cache_len, heads_loc, head_dim)
    v_local = v_cache.reshape(layers, row_count, cache_len, heads_loc, head_dim)
    wqkv_local = w_qkv.reshape(layers, model_width, 3, heads_loc, head_dim)
    wout_local = w_out.reshape(layers, heads_loc, head_dim, model_width)
    cos_tab, sin_tab = rope_tables(c_len, head_dim)
    cache_pos = jnp.arange(cache_len)
    visible = (cache_pos[None, :] < c_len[:, None])[:, None, :]
    write_at = (cache_pos[None, :] == c_len[:, None])[:, :, None, None]
    k_next = []
    v_next = []
    for layer_idx in range(layers):
        normed = rms_norm(tokens, gains[layer_idx, 0])
        qkv_out = jnp.einsum('bd,dkhe->bkhe', normed, wqkv_local[layer_idx], preferred_element_type=jnp.float32)
        queries = apply_rope(qkv_out[:, 0], cos_tab, sin_tab).astype(jnp.bfloat16)
        k_tok = apply_rope(qkv_out[:, 1], cos_tab, sin_tab).astype(jnp.bfloat16)
        v_tok = qkv_out[:, 2].astype(jnp.bfloat16)
        context = decode_attention(queries, k_tok, v_tok, k_local[layer_idx], v_local[layer_idx], visible)
        part_sum = jnp.einsum('bhe,hed->bd', context, wout_local[layer_idx], preferred_element_type=jnp.float32)
        tokens = add_residual(tokens, lax.psum(part_sum, 'tp').astype(jnp.bfloat16))
        mlp_part = swiglu(tokens, gains[layer_idx, 1], w_gu[layer_idx], w_down[layer_idx])
        tokens = add_residual(tokens, lax.psum(mlp_part, 'tp').astype(jnp.bfloat16))
        k_next.append(jnp.where(write_at, k_tok[:, None], k_local[layer_idx]))
        v_next.append(jnp.where(write_at, v_tok[:, None], v_local[layer_idx]))
    return tokens, jnp.stack(k_next).reshape(k_cache.shape), jnp.stack(v_next).reshape(v_cache.shape)


def heads_to_rows(kv_local, tp_size):
    pair_kv, seq_len, heads_loc, head_dim = kv_local.shape
    by_block = kv_local.reshape(pair_kv, tp_size, seq_len // tp_size, heads_loc, head_dim)
    gathered = lax.all_to_all(by_block, 'tp', 1, 2)
    return gathered.reshape(pair_kv, seq_len // tp_size, tp_size * heads_loc, head_dim)


def rows_to_heads(kv_rows, tp_size):
    pair_kv, seq_part, heads_all, head_dim = kv_rows.shape
    grouped = kv_rows.reshape(pair_kv, seq_part, heads_all // tp_size, tp_size, head_dim)
    spread = lax.all_to_all(grouped, 'tp', 3, 1)
    return spread.reshape(pair_kv, tp_size * seq_part, heads_all // tp_size, head_dim)


def solution(mesh):
    tp_size = mesh.shape['tp']
    side_size = mesh.shape['side']
    partner_perm = [(src_idx, (src_idx + side_size // 2) % side_size) for src_idx in range(side_size)]
    inst_axes = ('pair', 'side')
    rows_spec = P(inst_axes, None)
    vec_spec = P(inst_axes)
    cache_spec = P(None, inst_axes, None, None, 'tp', None)
    prompt_spec = P(None, inst_axes, None, 'tp', None)
    in_specs = (rows_spec, vec_spec, P(None, None, None, 'tp', None), P(None, 'tp', None, None), P(None, None, 'tp', None), P(None, 'tp', None), P(None, None, None), rows_spec, cache_spec, cache_spec, vec_spec, P(None, None, None, None, 'tp', None), P(None, None, 'tp', None, None), P(None, None, 'tp', None), P(None, 'tp', None), P(None, None, None))
    out_specs = (rows_spec, rows_spec, prompt_spec, prompt_spec, cache_spec, cache_spec)

    def device_fn(prompt_x, s_len, w_qkv_pre, w_out_pre, w_gu_pre, w_down_pre, gain_pre, dec_tokens, k_cache, v_cache, c_len, w_qkv_dec, w_out_dec, w_gu_dec, w_down_dec, gain_dec):
        hidden, kv_layers = run_prefill(prompt_x[None], s_len, w_qkv_pre, w_out_pre, w_gu_pre, w_down_pre, gain_pre)
        installed = []
        for kv_layer in kv_layers:
            kv_rows = heads_to_rows(kv_layer[:, 0], tp_size)
            kv_rows = lax.ppermute(kv_rows, 'side', partner_perm)
            installed.append(rows_to_heads(kv_rows, tp_size))
        prompt_kv = jnp.stack(installed, axis=1)[:, :, :, :, None, :]
        dec_out, k_cache_new, v_cache_new = run_decode(dec_tokens, k_cache, v_cache, c_len, w_qkv_dec, w_out_dec, w_gu_dec, w_down_dec, gain_dec)
        return hidden[0], dec_out, prompt_kv[0], prompt_kv[1], k_cache_new, v_cache_new

    return jax.shard_map(device_fn, mesh=mesh, in_specs=in_specs, out_specs=out_specs, check_vma=False)
```

profile of v0, /device:TPU:0, one launch (start us, length us, event | category | flops | bytes accessed | tf_op | source)
XLA Modules:
  0.0 1546.4 jit_solution(6348986690221009438)
XLA Ops:
  4.1 11.5 fusion.233
  17.8 2.4 slice_bitcast_fusion.9
  22.3 2.5 slice_bitcast_fusion.8
  26.2 7.2 fusion.234
  33.4 10.6 copy.224
  44.0 3.2 fusion.18
  47.5 9.0 fusion.83
  56.9 2.3 copy-done.9
  61.2 1.5 fusion.133
  62.7 11.6 fusion.237
  74.3 13.7 convolution_bitcast_fusion.1
  88.1 288.8 %all-reduce.8 = (bf16[1,1024,2048]{2,1,0:T(8,128)(2,1)}, bf16[8,2048]{1,0:T(8,128)(2,1)S(1)}) all-reduce(f32[1,1024,2048]{2,1,0:T(8,128)} %convolution_bitcast_fusion.1, f32[8,2048]{1,0:T(8,128)S(1)} %convolution_bitcast_fusion.3), channel_id=1, replica_groups=mesh['pair'=2,'tp'=4,'side'=4] {'tp'}, use_global_device_ids=true, to_apply=%region_3.4 | all-reduce | flops 2113536 | bytes 12681216 | tf_op jit(solution)/shard_map/psum | solution.py:84
  377.1 6.0 fusion.98
  383.1 3.6 fusion.53
  386.9 2.0 fusion.21
  389.0 16.2 %convert_bitcast_fusion.2 = bf16[1,1024,2,1376]{1,3,2,0:T(8,128)(2,1)S(1)} fusion(bf16[2,2,1376,2048]{3,2,1,0:T(8,128)(2,1)} %param.20, bf16[1,1024,2048]{2,1,0:T(8,128)(2,1)S(1)} %get-tuple-element.39, f32[2048]{0:T(1024)S(1)} %bitcast.353, f32[1024]{0:T(1024)S(1)} %add_rsqrt_fusion.2), kind=kOutput, calls=%fused_computation.84 | convolution fusion | flops 11553931264 | bytes 21114880 | tf_op jit(solution)/shard_map/...d,kfd->...kf/dot_general | solution.py:39
  405.2 11.4 fusion.69
  416.7 282.1 %all-reduce.9 = (bf16[1,1024,2048]{2,1,0:T(8,128)(2,1)}, bf16[8,2048]{1,0:T(8,128)(2,1)S(1)}) all-reduce(f32[1,1024,2048]{2,1,0:T(8,128)} %fusion.69, f32[8,2048]{1,0:T(8,128)S(1)} %fusion.53), channel_id=1, replica_groups=mesh['pair'=2,'tp'=4,'side'=4] {'tp'}, use_global_device_ids=true, to_apply=%region_5.6 | all-reduce | flops 2113536 | bytes 12681216 | tf_op jit(solution)/shard_map/psum | solution.py:86
  698.8 7.5 fusion.25
  706.3 10.6 copy.225
  716.9 10.2 fusion.79
  727.4 2.4 copy-done.10
  730.0 1.7 fusion.135
  734.7 1.6 copy.183
  736.3 1.6 convert_element_type.516
  737.9 1.7 copy.184
  739.6 2.0 pad_maximum_fusion.2
  741.6 4.1 all-to-all-start.2
  748.1 2.7 slice.499
  751.0 3.7 fusion.41
  754.8 1.6 copy.176
  756.4 2.3 copy.177
  758.7 2.6 convert_element_type.515
  761.3 2.4 copy.178
  763.9 2.4 fusion.111
  766.8 2.0 fusion.109
  769.2 11.8 fusion.238
  781.0 13.7 convolution_bitcast_fusion
  794.7 280.7 %all-reduce.10 = (bf16[1,1024,2048]{2,1,0:T(8,128)(2,1)}, bf16[8,2048]{1,0:T(8,128)(2,1)S(1)}) all-reduce(f32[1,1024,2048]{2,1,0:T(8,128)} %convolution_bitcast_fusion, f32[8,2048]{1,0:T(8,128)S(1)} %convolution_bitcast_fusion.2), channel_id=1, replica_groups=mesh['pair'=2,'tp'=4,'side'=4] {'tp'}, use_global_device_ids=true, to_apply=%region_9.10 | all-reduce | flops 2113536 | bytes 12681216 | tf_op jit(solution)/shard_map/psum | solution.py:84
  1075.6 3.7 pad_maximum_fusion.1
  1079.3 4.2 fusion.29
  1083.6 2.0 copy-done.2
  1085.6 16.7 %convert_bitcast_fusion.1 = bf16[1,1024,2,1376]{1,3,2,0:T(8,128)(2,1)} fusion(bf16[2,2,1376,2048]{3,2,1,0:T(8,128)(2,1)} %param.20, bf16[1,1024,2048]{2,1,0:T(8,128)(2,1)S(1)} %get-tuple-element.29, f32[2048]{0:T(1024)S(1)} %bitcast.351, f32[1024]{0:T(1024)S(1)} %add_rsqrt_fusion), kind=kOutput, calls=%fused_computation.83 | convolution fusion | flops 11553931264 | bytes 21114880 | tf_op jit(solution)/shard_map/...d,kfd->...kf/dot_general | solution.py:39
  1102.3 5.4 all-to-all-start
  1107.7 6.0 fusion.101
  1113.7 3.6 fusion.51
  1117.3 1.5 copy.185
  1118.8 4.0 collective-permute-start.1
  1122.9 9.9 fusion.72
  1132.8 18.3 %all-to-all-done = bf16[2,4,256,1,4,128]{5,2,4,0,3,1:T(8,128)(2,1)} async-done(((bf16[2,4,256,1,4,128]{5,2,4,0,3,1:T(8,128)(2,1)}), bf16[2,4,256,1,4,128]{5,2,4,0,3,1:T(8,128)(2,1)}, u32[]{:S(2)}, u32[]{:S(2)}) %all-to-all-start) | async-done | bytes 2097184 | tf_op jit(solution)/shard_map/all_to_all | solution.py:127
  1151.0 3.1 copy.179
  1154.2 5.3 collective-permute-start
  1159.5 9.8 collective-permute-done.1
  1170.8 5.1 all-to-all-start.3
  1175.8 309.1 %all-reduce.11 = (bf16[1,1024,2048]{2,1,0:T(8,128)(2,1)}, bf16[8,2048]{1,0:T(8,128)(2,1)S(1)}) all-reduce(f32[1,1024,2048]{2,1,0:T(8,128)} %fusion.72, f32[8,2048]{1,0:T(8,128)S(1)} %fusion.51), channel_id=1, replica_groups=mesh['pair'=2,'tp'=4,'side'=4] {'tp'}, use_global_device_ids=true, to_apply=%region_11.12 | all-reduce | flops 2113536 | bytes 12681216 | tf_op jit(solution)/shard_map/psum | solution.py:86
  1485.0 3.1 copy.180
  1488.2 6.9 all-to-all-start.1
  1496.5 7.5 bitcast_select_fusion.1
  1504.0 7.6 maximum_bitcast_fusion
  1511.5 4.0 fusion.75
  1517.0 20.8 %all-to-all-done.1 = bf16[2,1,256,4,4,128]{5,2,3,0,1,4:T(8,128)(2,1)} async-done(((bf16[2,1,256,4,4,128]{5,2,3,0,1,4:T(8,128)(2,1)}), bf16[2,1,256,4,4,128]{5,2,3,0,1,4:T(8,128)(2,1)}, u32[]{:S(2)}, u32[]{:S(2)}) %all-to-all-start.1) | async-done | bytes 2097184 | tf_op jit(solution)/shard_map/all_to_all | solution.py:134
  1537.9 1.7 copy.181
  1540.1 2.9 copy.192
  1543.0 2.9 copy.193
  (151 shorter events, 23.5 us)
Async XLA Ops:
  2.6 19.5 %copy-start.24 = (pred[8,256]{1,0:T(8,128)(4,1)}, pred[8,256]{1,0:T(8,128)(4,1)S(1)}, u32[]{:S(2)}) copy-start(pred[8,256]{1,0:T(8,128)(4,1)S(1)} %get-tuple-element.107) | copy-start | bytes 6148
  4.1 11.5 copy-start.22
  4.1 22.1 %slice-start = ((s8[12582912]{0:T(1024)(128)(4,1)}), s8[4194304]{0:T(1024)(128)(4,1)S(1)}, s32[]{:S(2)}) async-start(s8[12582912]{0:T(1024)(128)(4,1)} %bitcast.328), calls=%async_computation.4 | async-start | bytes 8388608
  4.1 22.2 %slice-start.1 = ((s8[12582912]{0:T(1024)(128)(4,1)}), s8[4194304]{0:T(1024)(128)(4,1)S(1)}, s32[]{:S(2)}) async-start(s8[12582912]{0:T(1024)(128)(4,1)} %bitcast.328), calls=%async_computation.5 | async-start | bytes 8388608
  15.6 2.2 copy-start.1
  16.7 8.4 copy-start.23
  17.8 4.5 copy-start
  17.8 8.4 slice-start.2
  20.3 1.9 copy-start.26
  20.3 1.9 copy-start.28
  22.2 2.9 copy-start.12
  24.7 0.9 copy-start.31
  44.0 3.4 copy-start.4
  56.5 2.6 copy-start.9
  61.2 13.1 copy-start.21
  62.7 11.6 copy-start.17
  62.7 11.6 copy-start.19
  377.0 9.6 copy-start.14
  383.0 3.9 copy-start.5
  388.9 16.3 %copy-start.7 = (bf16[1,1024,2048]{2,1,0:T(8,128)(2,1)}, bf16[1,1024,2048]{2,1,0:T(8,128)(2,1)S(1)}, u32[]{:S(2)}) copy-start(bf16[1,1024,2048]{2,1,0:T(8,128)(2,1)S(1)} %get-tuple-element.39) | copy-start | bytes 12582916
  727.1 2.7 copy-start.10
  731.7 0.8 copy-start.16
  731.7 1.9 copy-start.15
  741.6 4.2 copy-start.20
  741.6 5.3 copy-start.18
  741.6 9.4 copy-start.30
  741.6 360.7 %all-to-all-start.2 = ((bf16[2,4,256,1,4,128]{5,2,4,0,3,1:T(8,128)(2,1)}), bf16[2,4,256,1,4,128]{5,2,4,0,3,1:T(8,128)(2,1)S(1)}, u32[]{:S(2)}, u32[]{:S(2)}) async-start(bf16[2,4,256,1,4,128]{5,2,4,0,3,1:T(8,128)(2,1)} %pad_maximum_fusion.2), calls=%async_computation.2 | async-start | bytes 4194304 | tf_op jit(solution)/shard_map/all_to_all | solution.py:127
  754.8 8.9 copy-start.27
  754.8 8.9 copy-start.29
  756.4 9.9 copy-start.25
  763.7 5.1 copy-start.13
  1075.5 3.8 copy-start.6
  1079.3 6.2 copy-start.35
  1083.5 2.0 copy-start.2
  1102.3 5.4 copy-start.33
  1102.3 48.7 %all-to-all-start = ((bf16[2,4,256,1,4,128]{5,2,4,0,3,1:T(8,128)(2,1)}), bf16[2,4,256,1,4,128]{5,2,4,0,3,1:T(8,128)(2,1)}, u32[]{:S(2)}, u32[]{:S(2)}) async-start(bf16[2,4,256,1,4,128]{5,2,4,0,3,1:T(8,128)(2,1)} %pad_maximum_fusion.1), calls=%async_computation | async-start | bytes 4194304 | tf_op jit(solution)/shard_map/all_to_all | solution.py:127
  1107.7 15.1 slice-start.3
  1107.7 15.1 slice-start.4
  1113.7 9.1 slice-start.5
  1113.7 9.1 copy-start.36
  1118.8 50.5 %collective-permute-start.1 = (bf16[2,256,16,128]{3,1,2,0:T(8,128)(2,1)}, bf16[2,256,16,128]{3,1,2,0:T(8,128)(2,1)S(1)}, u32[]{:S(2)}, u32[]{:S(2)}) collective-permute-start(bf16[2,256,16,128]{3,1,2,0:T(8,128)(2,1)} %bitcast.113), channel_id=1, source_target_pairs={{0,2},{1,3},{2,0},{3,1},{4,6},{5,7},{6,4},{7,5},{8,10},{9,11},{10,... | collective-permute-start | bytes 6291464 | tf_op jit(solution)/shard_map/ppermute | solution.py:155
  1154.2 330.9 %collective-permute-start = (bf16[2,256,16,128]{3,1,2,0:T(8,128)(2,1)}, bf16[2,256,16,128]{3,1,2,0:T(8,128)(2,1)}, u32[]{:S(2)}, u32[]{:S(2)}) collective-permute-start(bf16[2,256,16,128]{3,1,2,0:T(8,128)(2,1)} %bitcast.106), channel_id=1, source_target_pairs={{0,2},{1,3},{2,0},{3,1},{4,6},{5,7},{6,4},{7,5},{8,10},{9,11},{10,... | collective-permute-start | bytes 6291464 | tf_op jit(solution)/shard_map/ppermute | solution.py:155
  1170.8 317.4 %all-to-all-start.3 = ((bf16[2,1,256,4,4,128]{5,2,3,0,1,4:T(8,128)(2,1)}), bf16[2,1,256,4,4,128]{5,2,3,0,1,4:T(8,128)(2,1)S(1)}, u32[]{:S(2)}, u32[]{:S(2)}) async-start(bf16[2,1,256,4,4,128]{5,2,3,0,1,4:T(8,128)(2,1)} %copy.186), calls=%async_computation.3 | async-start | bytes 4194304 | tf_op jit(solution)/shard_map/all_to_all | solution.py:134
  1175.8 309.2 %copy-start.32 = (bf16[8,4,128]{2,0,1:T(8,128)(2,1)S(1)}, bf16[8,4,128]{2,0,1:T(8,128)(2,1)}, u32[]{:S(2)}) copy-start(bf16[8,4,128]{2,0,1:T(8,128)(2,1)} %get-tuple-element.41) | copy-start | bytes 24580
  1485.0 11.4 copy-start.34
  1488.2 49.7 %all-to-all-start.1 = ((bf16[2,1,256,4,4,128]{5,2,3,0,1,4:T(8,128)(2,1)}), bf16[2,1,256,4,4,128]{5,2,3,0,1,4:T(8,128)(2,1)}, u32[]{:S(2)}, u32[]{:S(2)}) async-start(bf16[2,1,256,4,4,128]{5,2,3,0,1,4:T(8,128)(2,1)} %copy.180), calls=%async_computation.1 | async-start | bytes 4194304 | tf_op jit(solution)/shard_map/all_to_all | solution.py:134
  1503.9 7.6 copy-start.3
  1504.0 7.6 copy-start.11
  1517.0 22.6 %copy-start.8 = (bf16[2,1,256,4,4,128]{5,2,4,3,0,1:T(8,128)(2,1)S(1)}, bf16[2,1,256,4,4,128]{5,2,4,3,0,1:T(8,128)(2,1)}, u32[]{:S(2)}) copy-start(bf16[2,1,256,4,4,128]{5,2,4,3,0,1:T(8,128)(2,1)} %copy.187) | copy-start | bytes 6291460
where the time goes:
time: 1560 us; the launch traced here: 1550 us
  blocking collectives  1160 us (74%)
  matrix products  154 us (10%)
  local copies, waits for them, and re-layouts  97 us (6%)
  other arithmetic  51.9 us (3%)
  waiting for transfers between devices  48.9 us (3%)
  starting transfers between devices  30.9 us (2%)
    psum x2, blocking collectives, run_prefill(): hidden = add_residual(hidden, lax.psum(mlp_part, 'tp').astype(jnp.bfloat16))  591 us
    psum x2, blocking collectives, run_prefill(): hidden = add_residual(hidden, lax.psum(part_sum, 'tp').astype(jnp.bfloat16))  570 us
    dot_general x4, matrix products, swiglu(): jnp.einsum('...d,kfd->...kf', normed, w_gu, preferred_element_type=jnp.fl...  44.9 us
    unnamed x90, local copies, waits for them, and re-layouts  36.3 us
  transfers between devices with their start and end apart: 6, of which 3 were waited for; matrix products, arithmetic and copies ran while one was open for 8% of the time, Pallas kernels for 0%

commit v1 on v0

v1 whole, which is shorter than its diff:
```python
import jax
import jax.numpy as jnp
from jax import lax
from jax.experimental import pallas as pl
from jax.experimental.pallas import tpu as pltpu
from jax.sharding import PartitionSpec as P

EPSILON = 1e-6
THETA = 10000.0
MASKED = -1e30
CTX_ROWS = 128
SUM_ROWS = 32
DOT_ROWS = 128
DOT_COLS = 512
VMEM_BYTES = 56 * 1024 * 1024
MESH = pl.DeviceIdType.MESH


def greet(me, tp_size):
    barrier = pltpu.get_barrier_semaphore()
    for off in range(1, tp_size):
        pl.semaphore_signal(barrier, inc=1, device_id={'tp': lax.rem(me + off, tp_size)}, device_id_type=MESH)
    pl.semaphore_wait(barrier, tp_size - 1)


def to_peer(src, dst, send_sem, recv_sem, peer):
    return pltpu.make_async_remote_copy(src_ref=src, dst_ref=dst, send_sem=send_sem, recv_sem=recv_sem, device_id={'tp': peer}, device_id_type=MESH)


def share_small(me, tp_size, part_ref, held, send_sems, recv_sems):
    for off in range(1, tp_size):
        peer = lax.rem(me + off, tp_size)
        to_peer(part_ref, held.at[me], send_sems.at[off - 1], recv_sems.at[me], peer).start()


def sum_small(me, tp_size, part_ref, held, send_sems, recv_sems, out_ref):
    for off in range(1, tp_size):
        peer = lax.rem(me + off, tp_size)
        copy = to_peer(part_ref, held.at[peer], send_sems.at[off - 1], recv_sems.at[peer], peer)
        copy.wait_send()
        copy.wait_recv()
    held[me] = part_ref[...]
    total = held[0]
    for idx in range(1, tp_size):
        total = total + held[idx]
    out_ref[...] = total.astype(out_ref.dtype)


def ctx_kernel(tp_size, ctx_ref, part_ref, full_ref, small_ref, held, up_send, up_recv, dn_send, dn_recv, sm_send, sm_recv):
    me = lax.axis_index('tp')
    last = tp_size - 1
    chunks = ctx_ref.shape[0] // CTX_ROWS
    greet(me, tp_size)
    share_small(me, tp_size, part_ref, held, sm_send, sm_recv)

    def rows_of(chunk):
        return pl.ds(pl.multiple_of(chunk * CTX_ROWS, CTX_ROWS), CTX_ROWS)

    def tick(step, carry):
        for back in range(tp_size):
            chunk = step - back
            inside = (chunk >= 0) & (chunk < chunks)
            for sign, send, recv in ((1, up_send, up_recv), (-1, dn_send, dn_recv)):
                shard = me - sign * back
                peer = me + sign
                has = inside & (shard >= 0) & (shard <= last)
                more = has & (peer >= 0) & (peer <= last)
                rows = rows_of(chunk)
                if back == 0:
                    @pl.when(more)
                    def _():
                        to_peer(ctx_ref.at[rows], full_ref.at[me, rows], send.at[0, chunk], recv.at[0, chunk], peer).start()
                else:
                    @pl.when(has)
                    def _():
                        to_peer(ctx_ref.at[rows], full_ref.at[shard, rows], send.at[back - 1, chunk], recv.at[back - 1, chunk], me).wait_recv()
                    if back < last:
                        @pl.when(more)
                        def _():
                            to_peer(full_ref.at[shard, rows], full_ref.at[shard, rows], send.at[back, chunk], recv.at[back, chunk], peer).start()
        return carry

    lax.fori_loop(0, chunks + last, tick, 0)
    full_ref[me] = ctx_ref[...]

    def drain(chunk, carry):
        for back in range(last):
            for sign, send, recv in ((1, up_send, up_recv), (-1, dn_send, dn_recv)):
                shard = me - sign * back
                peer = me + sign

                @pl.when((shard >= 0) & (shard <= last) & (peer >= 0) & (peer <= last))
                def _():
                    to_peer(ctx_ref.at[rows_of(chunk)], full_ref.at[me, rows_of(chunk)], send.at[back, chunk], recv.at[back, chunk], peer).wait_send()
        return carry

    lax.fori_loop(0, chunks, drain, 0)
    sum_small(me, tp_size, part_ref, held, sm_send, sm_recv, small_ref)


def gather_ctx(ctx, small_part, tp_size):
    rows, width = ctx.shape
    chunks = rows // CTX_ROWS
    last = tp_size - 1
    vmem = pl.BlockSpec(memory_space=pltpu.VMEM)
    return pl.pallas_call(
        lambda *refs: ctx_kernel(tp_size, *refs),
        out_shape=(jax.ShapeDtypeStruct((tp_size, rows, width), ctx.dtype), jax.ShapeDtypeStruct(small_part.shape, jnp.bfloat16)),
        in_specs=[vmem, vmem],
        out_specs=(vmem, vmem),
        scratch_shapes=[pltpu.VMEM((tp_size,) + small_part.shape, jnp.float32)] + [pltpu.SemaphoreType.DMA((last, chunks))] * 4 + [pltpu.SemaphoreType.DMA((last,)), pltpu.SemaphoreType.DMA((tp_size,))],
        compiler_params=pltpu.CompilerParams(collective_id=0, has_side_effects=True, vmem_limit_bytes=VMEM_BYTES),
        cost_estimate=pl.CostEstimate(flops=70_000_000_000, bytes_accessed=rows * width * 10, transcendentals=0),
        name='ctx_gather',
    )(ctx, small_part)


def sum_kernel(tp_size, act_ref, wd_ref, hid_ref, part_ref, out_ref, small_ref, total, came, held, up_send, up_recv, dn_send, dn_recv, gu_send, gu_recv, gd_send, gd_recv, sm_send, sm_recv):
    me = lax.axis_index('tp')
    last = tp_size - 1
    half = hid_ref.shape[0] // 2
    chunks = half // SUM_ROWS
    per_dot = DOT_ROWS // SUM_ROWS
    width = hid_ref.shape[1]
    greet(me, tp_size)
    share_small(me, tp_size, part_ref, held, sm_send, sm_recv)
    streams = ((1, half, up_send, up_recv, gu_send, gu_recv), (-1, 0, dn_send, dn_recv, gd_send, gd_recv))

    def tick(step, carry):
        @pl.when((lax.rem(step, per_dot) == 0) & (step < chunks))
        def _():
            for base in (half, 0):
                rows = pl.ds(pl.multiple_of(base + step * SUM_ROWS, SUM_ROWS), DOT_ROWS)

                def columns(idx, inner):
                    cols = pl.ds(pl.multiple_of(idx * DOT_COLS, DOT_COLS), DOT_COLS)
                    total[rows, cols] = jnp.dot(act_ref[rows, :], wd_ref[:, cols], preferred_element_type=jnp.float32)
                    return inner

                lax.fori_loop(0, width // DOT_COLS, columns, 0)

        for sign, base, send, recv, g_send, g_recv in streams:
            place = me if sign == 1 else last - me
            chunk = step - place
            rows = pl.ds(pl.multiple_of(base + chunk * SUM_ROWS, SUM_ROWS), SUM_ROWS)
            inside = (chunk >= 0) & (chunk < chunks)
            nxt = me + sign
            prev = me - sign

            @pl.when(inside & (place > 0))
            def _():
                to_peer(total.at[rows], came.at[rows], send.at[chunk], recv.at[chunk], me).wait_recv()

                @pl.when(place < last)
                def _():
                    total[rows, :] = total[rows, :] + came[rows, :]

                @pl.when(place == last)
                def _():
                    update = (total[rows, :] + came[rows, :]).astype(jnp.bfloat16).astype(jnp.float32)
                    out_ref[rows, :] = (hid_ref[rows, :].astype(jnp.float32) + update).astype(jnp.bfloat16)
                    to_peer(out_ref.at[rows], out_ref.at[rows], g_send.at[chunk], g_recv.at[chunk], prev).start()

            @pl.when(inside & (place < last))
            def _():
                to_peer(total.at[rows], came.at[rows], send.at[chunk], recv.at[chunk], nxt).start()

        for sign, base, send, recv, g_send, g_recv in streams:
            place = me if sign == 1 else last - me
            chunk = step - last - (last - place)
            rows = pl.ds(pl.multiple_of(base + chunk * SUM_ROWS, SUM_ROWS), SUM_ROWS)
            prev = me - sign

            @pl.when((chunk >= 0) & (chunk < chunks) & (place < last))
            def _():
                to_peer(out_ref.at[rows], out_ref.at[rows], g_send.at[chunk], g_recv.at[chunk], me).wait_recv()

                @pl.when(place > 0)
                def _():
                    to_peer(out_ref.at[rows], out_ref.at[rows], g_send.at[chunk], g_recv.at[chunk], prev).start()
        return carry

    lax.fori_loop(0, chunks + 2 * last, tick, 0)

    def drain(chunk, carry):
        for sign, base, send, recv, g_send, g_recv in streams:
            place = me if sign == 1 else last - me
            rows = pl.ds(pl.multiple_of(base + chunk * SUM_ROWS, SUM_ROWS), SUM_ROWS)

            @pl.when(place < last)
            def _():
                to_peer(total.at[rows], came.at[rows], send.at[chunk], recv.at[chunk], me + sign).wait_send()

            @pl.when(place > 0)
            def _():
                to_peer(out_ref.at[rows], out_ref.at[rows], g_send.at[chunk], g_recv.at[chunk], me - sign).wait_send()
        return carry

    lax.fori_loop(0, chunks, drain, 0)
    sum_small(me, tp_size, part_ref, held, sm_send, sm_recv, small_ref)


def down_and_sum(act, w_down, hidden, small_part, tp_size):
    rows, width = hidden.shape
    chunks = rows // 2 // SUM_ROWS
    vmem = pl.BlockSpec(memory_space=pltpu.VMEM)
    return pl.pallas_call(
        lambda *refs: sum_kernel(tp_size, *refs),
        out_shape=(jax.ShapeDtypeStruct(hidden.shape, hidden.dtype), jax.ShapeDtypeStruct(small_part.shape, jnp.bfloat16)),
        in_specs=[vmem] * 4,
        out_specs=(vmem, vmem),
        scratch_shapes=[pltpu.VMEM((rows, width), jnp.float32), pltpu.VMEM((rows, width), jnp.float32), pltpu.VMEM((tp_size,) + small_part.shape, jnp.float32)] + [pltpu.SemaphoreType.DMA((chunks,))] * 8 + [pltpu.SemaphoreType.DMA((tp_size - 1,)), pltpu.SemaphoreType.DMA((tp_size,))],
        compiler_params=pltpu.CompilerParams(collective_id=1, has_side_effects=True, vmem_limit_bytes=VMEM_BYTES),
        cost_estimate=pl.CostEstimate(flops=150_000_000_000, bytes_accessed=rows * width * 10, transcendentals=0),
        name='down_sum',
    )(act, w_down, hidden, small_part)


def rms_norm(hidden, gain_vec):
    hid_f32 = hidden.astype(jnp.float32)
    inv_rms = lax.rsqrt(jnp.mean(hid_f32 * hid_f32, axis=-1, keepdims=True) + EPSILON)
    return (hid_f32 * inv_rms * gain_vec).astype(jnp.bfloat16)


def add_residual(hidden, update):
    return (hidden.astype(jnp.float32) + update.astype(jnp.float32)).astype(jnp.bfloat16)


def rope_tables(positions, head_dim):
    half_dim = head_dim // 2
    inv_freq = THETA ** (-jnp.arange(half_dim, dtype=jnp.float32) * 2.0 / head_dim)
    angles = positions.astype(jnp.float32)[:, None] * inv_freq[None, :]
    return jnp.cos(angles), jnp.sin(angles)


def apply_rope(values_in, cos_tab, sin_tab):
    half_dim = values_in.shape[-1] // 2
    lower_half = values_in[..., :half_dim]
    upper_half = values_in[..., half_dim:]
    cos_b = cos_tab[:, None, :]
    sin_b = sin_tab[:, None, :]
    return jnp.concatenate([lower_half * cos_b - upper_half * sin_b, upper_half * cos_b + lower_half * sin_b], axis=-1)


def swiglu(hidden, gain_vec, w_gu):
    normed = rms_norm(hidden, gain_vec)
    gate_up = jnp.einsum('sd,kfd->skf', normed, w_gu, preferred_element_type=jnp.float32)
    gate_val = gate_up[..., 0, :].astype(jnp.bfloat16).astype(jnp.float32)
    up_val = gate_up[..., 1, :].astype(jnp.bfloat16).astype(jnp.float32)
    return (jax.nn.silu(gate_val) * up_val).astype(jnp.bfloat16)


def prompt_attention(queries, keys_in, values_in, allowed):
    attn_scale = queries.shape[-1] ** -0.5
    scores = jnp.einsum('qhe,khe->hqk', queries, keys_in, preferred_element_type=jnp.float32) * attn_scale
    scores = jnp.where(allowed[None], scores, MASKED)
    prob_bf = jax.nn.softmax(scores, axis=-1).astype(jnp.bfloat16)
    return jnp.einsum('hqk,khe->qhe', prob_bf, values_in, preferred_element_type=jnp.float32).astype(jnp.bfloat16)


def decode_attention(queries, k_tok, v_tok, k_layer, v_layer, visible):
    attn_scale = queries.shape[-1] ** -0.5
    cache_scores = jnp.einsum('bhe,bthe->bht', queries, k_layer, preferred_element_type=jnp.float32) * attn_scale
    cache_scores = jnp.where(visible, cache_scores, MASKED)
    self_score = jnp.einsum('bhe,bhe->bh', queries, k_tok, preferred_element_type=jnp.float32) * attn_scale
    row_max = jnp.maximum(jnp.max(cache_scores, axis=-1), self_score)
    cache_exp = jnp.exp(cache_scores - row_max[..., None])
    self_exp = jnp.exp(self_score - row_max)
    denominator = jnp.sum(cache_exp, axis=-1) + self_exp
    cache_prob = (cache_exp / denominator[..., None]).astype(jnp.bfloat16)
    self_prob = (self_exp / denominator).astype(jnp.bfloat16).astype(jnp.float32)
    context = jnp.einsum('bht,bthe->bhe', cache_prob, v_layer, preferred_element_type=jnp.float32) + self_prob[..., None] * v_tok.astype(jnp.float32)
    return context.astype(jnp.bfloat16)


def run_layers(prompt, s_valid, w_qkv_pre, wo_full, w_gu_pre, w_down_pre, gains_pre, tokens, k_cache, v_cache, c_len, w_qkv_dec, w_out_dec, w_gu_dec, w_down_dec, gains_dec, partner_perm, tp_size):
    layers, row_count, cache_len, heads_loc, _, head_dim = k_cache.shape
    width = tokens.shape[1]
    seq_len = prompt.shape[0]
    k_local = k_cache.reshape(layers, row_count, cache_len, heads_loc, head_dim)
    v_local = v_cache.reshape(layers, row_count, cache_len, heads_loc, head_dim)
    wqkv_local = w_qkv_dec.reshape(layers, width, 3, heads_loc, head_dim)
    wout_local = w_out_dec.reshape(layers, heads_loc, head_dim, width)
    cos_dec, sin_dec = rope_tables(c_len, head_dim)
    cache_pos = jnp.arange(cache_len)
    visible = (cache_pos[None, :] < c_len[:, None])[:, None, :]
    write_at = (cache_pos[None, :] == c_len[:, None])[:, :, None, None]
    positions = jnp.arange(seq_len)
    cos_pre, sin_pre = rope_tables(positions, head_dim)
    allowed = (positions[None, :] <= positions[:, None]) & (positions[None, :] < s_valid[:, None])
    hidden = prompt
    installed, k_next, v_next = [], [], []
    for layer_idx in range(layers):
        normed = rms_norm(hidden, gains_pre[layer_idx, 0])
        qkv_out = jnp.einsum('sd,dkhe->skhe', normed, w_qkv_pre[layer_idx], preferred_element_type=jnp.float32)
        queries = apply_rope(qkv_out[:, 0], cos_pre, sin_pre).astype(jnp.bfloat16)
        keys_new = apply_rope(qkv_out[:, 1], cos_pre, sin_pre).astype(jnp.bfloat16)
        values_new = qkv_out[:, 2].astype(jnp.bfloat16)
        context = prompt_attention(queries, keys_new, values_new, allowed).reshape(seq_len, -1)

        normed_tok = rms_norm(tokens, gains_dec[layer_idx, 0])
        qkv_tok = jnp.einsum('bd,dkhe->bkhe', normed_tok, wqkv_local[layer_idx], preferred_element_type=jnp.float32)
        q_tok = apply_rope(qkv_tok[:, 0], cos_dec, sin_dec).astype(jnp.bfloat16)
        k_tok = apply_rope(qkv_tok[:, 1], cos_dec, sin_dec).astype(jnp.bfloat16)
        v_tok = qkv_tok[:, 2].astype(jnp.bfloat16)
        ctx_tok = decode_attention(q_tok, k_tok, v_tok, k_local[layer_idx], v_local[layer_idx], visible)
        part_tok = jnp.einsum('bhe,hed->bd', ctx_tok, wout_local[layer_idx], preferred_element_type=jnp.float32)
        k_next.append(jnp.where(write_at, k_tok[:, None], k_local[layer_idx]))
        v_next.append(jnp.where(write_at, v_tok[:, None], v_local[layer_idx]))

        ctx_full, attn_tok = gather_ctx(context, part_tok, tp_size)
        kv_new = lax.ppermute(jnp.stack([keys_new, values_new]), 'side', partner_perm)
        installed.append(lax.all_to_all(kv_new, 'tp', 2, 2, tiled=True))

        attn = jnp.einsum('zsf,zfd->sd', ctx_full, wo_full[layer_idx], preferred_element_type=jnp.float32)
        hidden = add_residual(hidden, attn.astype(jnp.bfloat16))
        act = swiglu(hidden, gains_pre[layer_idx, 1], w_gu_pre[layer_idx])
        tokens = add_residual(tokens, attn_tok)
        act_tok = swiglu(tokens, gains_dec[layer_idx, 1], w_gu_dec[layer_idx])
        mlp_tok = jnp.einsum('bf,fd->bd', act_tok, w_down_dec[layer_idx], preferred_element_type=jnp.float32)
        hidden, down_tok = down_and_sum(act, w_down_pre[layer_idx], hidden, mlp_tok, tp_size)
        tokens = add_residual(tokens, down_tok)
    k_new = jnp.stack(k_next).reshape(k_cache.shape)
    v_new = jnp.stack(v_next).reshape(v_cache.shape)
    return hidden, tokens, installed, k_new, v_new


def gather_wo(w_out, side_size, pair_size):
    layers, heads_loc, head_dim, width = w_out.shape
    rows = heads_loc * head_dim
    copies = side_size * pair_size
    part = rows // copies
    place = lax.axis_index('pair') * side_size + lax.axis_index('side')
    flat = w_out.reshape(layers, rows, width)
    mine = lax.dynamic_slice_in_dim(flat, place * part, part, axis=1)
    full = []
    for layer_idx in range(layers):
        everything = lax.all_gather(mine[layer_idx], ('tp', 'pair', 'side'), axis=0, tiled=True)
        full.append(everything.reshape(-1, rows, width))
    return full


def solution(mesh):
    tp_size = mesh.shape['tp']
    side_size = mesh.shape['side']
    pair_size = mesh.shape['pair']
    partner_perm = [(src_idx, (src_idx + side_size // 2) % side_size) for src_idx in range(side_size)]
    inst_axes = ('pair', 'side')
    rows_spec = P(inst_axes, None)
    vec_spec = P(inst_axes)
    cache_spec = P(None, inst_axes, None, None, 'tp', None)
    prompt_spec = P(None, inst_axes, None, 'tp', None)
    in_specs = (rows_spec, vec_spec, P(None, None, None, 'tp', None), P(None, 'tp', None, None), P(None, None, 'tp', None), P(None, 'tp', None), P(None, None, None), rows_spec, cache_spec, cache_spec, vec_spec, P(None, None, None, None, 'tp', None), P(None, None, 'tp', None, None), P(None, None, 'tp', None), P(None, 'tp', None), P(None, None, None))
    out_specs = (rows_spec, rows_spec, prompt_spec, prompt_spec, cache_spec, cache_spec)

    def device_fn(prompt_x, s_len, w_qkv_pre, w_out_pre, w_gu_pre, w_down_pre, gain_pre, dec_tokens, k_cache, v_cache, c_len, w_qkv_dec, w_out_dec, w_gu_dec, w_down_dec, gain_dec):
        wo_full = gather_wo(w_out_pre, side_size, pair_size)
        hidden, dec_out, installed, k_cache_new, v_cache_new = run_layers(prompt_x, s_len, w_qkv_pre, wo_full, w_gu_pre, w_down_pre, gain_pre, dec_tokens, k_cache, v_cache, c_len, w_qkv_dec, w_out_dec, w_gu_dec, w_down_dec, gain_dec, partner_perm, tp_size)
        prompt_kv = jnp.stack(installed, axis=1)[:, :, :, :, None, :]
        return hidden, dec_out, prompt_kv[0], prompt_kv[1], k_cache_new, v_cache_new

    return jax.shard_map(device_fn, mesh=mesh, in_specs=in_specs, out_specs=out_specs, check_vma=False)
```

time: 1560 us -> 891 us (0.57)
  blocking collectives: 1160 us -> 0 us
  Pallas kernels: 0 us -> 568 us
  waiting for transfers between devices: 48.9 us -> 0.08 us
  starting transfers between devices: 30.9 us -> 12.8 us
    psum x4 -> x0, blocking collectives: 1160 us -> none  [the longest x2 591 us: run_prefill(): hidden = add_residual(hidden, lax.psum(mlp_part, 'tp').astype(jnp.bfloat16))]
    pallas_call x0 -> x4, Pallas kernels: none -> 568 us  [the longest x2 373 us: down_and_sum(): pl.pallas_call(lambda *refs: sum_kernel(tp_size, *refs), out_shape=(jax.S...]
    all_to_all x4 -> x2, waiting for transfers between devices: 39.1 us -> 0.01 us  [run_layers(): installed.append(lax.all_to_all(kv_new, 'tp', 2, 2, tiled=True))]
    unnamed x90 -> x93, local copies, waits for them, and re-layouts: 36.3 us -> 38.4 us
  transfers between devices with their start and end apart: 6 -> 6, of which waited for: 3 -> 0; matrix products, arithmetic and copies ran while one was open for 8% -> 30% of each run, Pallas kernels for 0% -> 64%
where the time goes in v1:
time: 891 us; the launch traced here: 881 us
  Pallas kernels  568 us (64%)
  matrix products  151 us (17%)
  local copies, waits for them, and re-layouts  91.4 us (10%)
  other arithmetic  42.4 us (5%)
  between operations  15.9 us (2%)
  starting transfers between devices  12.8 us (1%)
    pallas_call x2, Pallas kernels, down_and_sum(): pl.pallas_call(lambda *refs: sum_kernel(tp_size, *refs), out_shape=(jax.S...  373 us
    pallas_call x2, Pallas kernels, gather_ctx(): pl.pallas_call(lambda *refs: ctx_kernel(tp_size, *refs), out_shape=(jax.S...  195 us
    dot_general x4, matrix products, swiglu(): jnp.einsum('sd,kfd->skf', normed, w_gu, preferred_element_type=jnp.float32)  48 us
    unnamed x93, local copies, waits for them, and re-layouts  38.4 us
    dot_general x2, matrix products, run_layers(): jnp.einsum('zsf,zfd->sd', ctx_full, wo_full[layer_idx], preferred_element...  26.8 us
    sub x2, matrix products, prompt_attention(): prob_bf = jax.nn.softmax(scores, axis=-1).astype(jnp.bfloat16)  21.8 us
    unnamed x2, matrix products  18.3 us
  transfers between devices with their start and end apart: 6, of which 0 were waited for; matrix products, arithmetic and copies ran while one was open for 30% of the time, Pallas kernels for 64%

profile of v1, /device:TPU:0, one launch (start us, length us, event | category | flops | bytes accessed | tf_op | source)
XLA Modules:
  0.0 881.4 jit_solution(13738844924209393577)
XLA Ops:
  7.2 1.9 constant_dynamic-slice_fusion.1
  9.2 11.9 %fusion.200 = (bf16[1,2048,3,4,128]{4,3,2,1,0:T(4,128)(2,1)}, bf16[1,2048,3,4,128]{4,3,2,1,0:T(4,128)(2,1)}) fusion(bf16[2,2048,3,4,128]{4,3,2,1,0:T(4,128)(2,1)} %param.18), kind=kLoop, calls=%fused_computation.308 | loop fusion | bytes 25165824 | tf_op jit(solution)/shard_map/slice | solution.py:295
  21.1 10.6 %copy.144 = bf16[1,2048,3,4,128]{1,4,3,2,0:T(8,128)(2,1)} copy(bf16[1,2048,3,4,128]{4,3,2,1,0:T(4,128)(2,1)} %get-tuple-element.49) | data formatting | bytes 12582912
  31.7 3.2 fusion.22
  35.0 1.0 multiply_cosine_fusion
  36.0 0.7 fusion.202
  36.7 9.0 %fusion.64 = f32[1024,1536]{0,1:S(1)} fusion(bf16[2048,1536]{0,1:T(8,128)(2,1)} %bitcast.254, bf16[1024,2048]{1,0:T(8,128)(2,1)S(1)} %copy-done.6, f32[2048]{0:T(1024)S(1)} %bitcast.277, f32[1024]{0:T(1024)S(1)} %add_rsqrt_fusion.3), kind=kOutput, calls=%fused_computation.85 | convolution fusion | flops 6450839552 | bytes 16789504
  46.3 2.1 copy-done.4
  48.3 1.7 subtract_convert_fusion.3
  50.2 3.1 collective-permute-start
  53.3 0.7 iota_compare_fusion.1
  54.6 10.1 %fusion.199 = (bf16[1,2048,3,4,1,128]{5,3,4,2,1,0:T(4,128)(2,1)}, bf16[1,2048,3,4,1,128]{5,3,4,2,1,0:T(4,128)(2,1)S(1)}) fusion(bf16[2,2048,3,4,1,128]{5,3,4,2,1,0:T(4,128)(2,1)} %param.27), kind=kLoop, calls=%fused_computation.307 | loop fusion | bytes 25165824 | tf_op jit(solution)/shard_map/slice | solution.py:302
  64.9 1.0 fusion.39
  66.0 0.9 copy-done.2
  66.9 2.4 slice_bitcast_fusion.15
  69.7 0.6 fusion.94
  70.7 2.8 slice_bitcast_fusion.14
  74.2 1.4 fusion.78
  75.6 11.7 %fusion.203 = (f32[4,1024]{1,0:T(4,128)S(1)}, f32[4,1024,1024]{1,2,0:T(8,128)}) fusion(pred[1024,1024]{0,1:T(8,128)(4,1)} %fusion.78, bf16[1024,4,64]{0,2,1:T(8,128)(2,1)S(1)} %get-tuple-element.78, bf16[1024,4,64]{0,2,1:T(8,128)(2,1)S(1)} %get-tuple-element.79, bf16[1024,4,64]{0,2,1:T(8,128)(2,1)} %get-tuple-element.73, ...), kind=kOutput, calls=%fused_computation.311 | convolution fusion | flops 1094714368 | bytes 19939328 | tf_op jit(solution)/shard_map/sub | solution.py:257
  87.3 7.7 fusion.101
  95.0 1.3 copy.140.refs_0_
  96.4 2.0 fusion.92
  98.3 2.7 convolution_bitcast_fusion.1.refs_1_
  101.0 119.9 %ctx_gather.2 = (bf16[4,1024,512]{2,1,0:T(8,128)(2,1)}, bf16[8,2048]{1,0:T(8,128)(2,1)}) custom-call(bf16[1024,512]{1,0:T(8,128)(2,1)} %copy.140.refs_0_, f32[8,2048]{1,0:T(8,128)} %convolution_bitcast_fusion.1.refs_1_), custom_call_target="tpu_custom_call" | custom-call | flops 70000001024 | bytes 5242880 | tf_op jit(solution)/shard_map/ctx_gather/pallas_call | solution.py:106
  220.9 0.9 fusion.112
  222.4 7.3 fusion.79
  229.7 0.6 copy.108
  230.3 10.6 %copy.146 = bf16[1,2048,3,4,128]{1,4,3,2,0:T(8,128)(2,1)} copy(bf16[1,2048,3,4,128]{4,3,2,1,0:T(4,128)(2,1)} %get-tuple-element.48) | data formatting | bytes 12582912
  241.0 4.1 fusion.52.refs_3_
  245.1 10.8 %slice_bitcast_fusion = (bf16[1376,2048]{1,0:T(8,128)(2,1)}, bf16[1376,2048]{1,0:T(8,128)(2,1)}) fusion(bf16[2,1376,2048]{2,1,0:T(8,128)(2,1)} %param.21), kind=kLoop, calls=%fused_computation.79 | loop fusion | bytes 22544384 | tf_op jit(solution)/shard_map/squeeze | solution.py:321
  255.8 3.1 copy.104
  258.9 4.6 all-to-all-start
  263.6 13.4 %fusion.16 = (f32[1024]{0:T(1024)S(1)}, bf16[1024,2048]{1,0:T(8,128)(2,1)S(1)}) fusion(bf16[4,1024,512]{2,1,0:T(8,128)(2,1)} %get-tuple-element.14, bf16[4,512,2048]{2,1,0:T(8,128)(2,1)} %bitcast.279, bf16[1024,2048]{1,0:T(8,128)(2,1)} %param.16), kind=kOutput, calls=%fused_computation.32 | convolution fusion | flops 8606710784 | bytes 20975616 | tf_op jit(solution)/shard_map/zsf,zfd->sd/dot_general | solution.py:315
  277.1 17.4 %fusion.56 = bf16[1024,2,1376]{2,0,1:T(8,128)(2,1)S(1)} fusion(bf16[2,2,1376,2048]{3,2,1,0:T(8,128)(2,1)} %param.20, bf16[1024,2048]{1,0:T(8,128)(2,1)S(1)} %get-tuple-element.119.refs_2_, f32[2048]{0:T(1024)S(1)} %bitcast.276, f32[1024]{0:T(1024)S(1)} %add_rsqrt_fusion.2), kind=kOutput, calls=%fused_computation.82 | convolution fusion | flops 11553931264 | bytes 21114880 | tf_op jit(solution)/shard_map/sd,kfd->skf/dot_general | solution.py:247
  294.5 2.9 fusion.49.refs_0_
  297.4 173.3 %down_sum.2 = (bf16[1024,2048]{1,0:T(8,128)(2,1)}, bf16[8,2048]{1,0:T(8,128)(2,1)}) custom-call(bf16[1024,1376]{1,0:T(8,128)(2,1)} %fusion.49.refs_0_, bf16[1376,2048]{1,0:T(8,128)(2,1)} %get-tuple-element.51.refs_1_, bf16[1024,2048]{1,0:T(8,128)(2,1)} %copy-done.43, f32[8,2048]{1,0:T(8,128)} %fusion.52.refs_3_), custom_call_target="tpu_custom_call" | custom-call | flops 149999992832 | bytes 20971520 | tf_op jit(solution)/shard_map/down_sum/pallas_call | solution.py:207
  470.7 3.2 fusion.26
  474.2 9.3 %fusion.62 = f32[1024,1536]{0,1:S(1)} fusion(bf16[2048,1536]{0,1:T(8,128)(2,1)} %bitcast.253, bf16[1024,2048]{1,0:T(8,128)(2,1)S(1)} %copy-done.8, f32[2048]{0:T(1024)S(1)} %bitcast.275, f32[1024]{0:T(1024)S(1)} %add_rsqrt_fusion.1), kind=kOutput, calls=%fused_computation.84 | convolution fusion | flops 6450839552 | bytes 16789504
  483.9 2.2 copy-done.5
  486.1 0.7 subtract_convert_fusion.1
  486.8 1.6 pad_maximum_fusion.2
  489.0 10.1 %fusion.204 = (f32[4,1024]{1,0:T(4,128)S(1)}, f32[4,1024,1024]{1,2,0:T(8,128)}) fusion(pred[1024,1024]{0,1:T(8,128)(4,1)S(1)} %copy-done.14, bf16[1024,4,64]{0,2,1:T(8,128)(2,1)S(1)} %get-tuple-element.76, bf16[1024,4,64]{0,2,1:T(8,128)(2,1)S(1)} %get-tuple-element.77, bf16[1024,4,64]{0,2,1:T(8,128)(2,1)S(1)} %get-tuple-element.69, ...), kind=kOutput, calls=%fused_computation.312 | convolution fusion | flops 1094714368 | bytes 19939328 | tf_op jit(solution)/shard_map/sub | solution.py:257
  499.1 7.7 fusion.100
  506.9 1.3 copy.142.refs_0_
  508.4 3.9 fusion.38
  512.5 0.7 fusion.163
  514.7 1.1 convolution_bitcast_fusion.refs_1_
  515.7 75.1 %ctx_gather.3 = (bf16[4,1024,512]{2,1,0:T(8,128)(2,1)}, bf16[8,2048]{1,0:T(8,128)(2,1)}) custom-call(bf16[1024,512]{1,0:T(8,128)(2,1)} %copy.142.refs_0_, f32[8,2048]{1,0:T(8,128)} %convolution_bitcast_fusion.refs_1_), custom_call_target="tpu_custom_call" | custom-call | flops 70000001024 | bytes 5242880 | tf_op jit(solution)/shard_map/ctx_gather/pallas_call | solution.py:106
  590.9 13.4 %fusion.19 = (f32[1024]{0:T(1024)S(1)}, bf16[1024,2048]{1,0:T(8,128)(2,1)S(1)}) fusion(bf16[4,1024,512]{2,1,0:T(8,128)(2,1)} %get-tuple-element.18, bf16[4,512,2048]{2,1,0:T(8,128)(2,1)} %bitcast.278, bf16[1024,2048]{1,0:T(8,128)(2,1)} %get-tuple-element.16), kind=kOutput, calls=%fused_computation.35 | convolution fusion | flops 8606710784 | bytes 20975616 | tf_op jit(solution)/shard_map/zsf,zfd->sd/dot_general | solution.py:315
  604.4 17.5 %fusion.59 = bf16[1024,2,1376]{2,0,1:T(8,128)(2,1)S(1)} fusion(bf16[2,2,1376,2048]{3,2,1,0:T(8,128)(2,1)} %param.20, bf16[1024,2048]{1,0:T(8,128)(2,1)S(1)} %get-tuple-element.123.refs_2_, f32[2048]{0:T(1024)S(1)} %bitcast.274, f32[1024]{0:T(1024)S(1)} %add_rsqrt_fusion), kind=kOutput, calls=%fused_computation.83 | convolution fusion | flops 11553931264 | bytes 21114880 | tf_op jit(solution)/shard_map/sd,kfd->skf/dot_general | solution.py:247
  622.1 5.8 fusion.82
  628.0 4.1 fusion.50.refs_3_
  632.1 2.9 fusion.48.refs_0_
  634.9 3.1 copy.105
  638.0 4.5 all-to-all-start.1
  642.6 199.6 %down_sum.3 = (bf16[1024,2048]{1,0:T(8,128)(2,1)}, bf16[8,2048]{1,0:T(8,128)(2,1)}) custom-call(bf16[1024,1376]{1,0:T(8,128)(2,1)} %fusion.48.refs_0_, bf16[1376,2048]{1,0:T(8,128)(2,1)} %get-tuple-element.50.refs_1_, bf16[1024,2048]{1,0:T(8,128)(2,1)} %copy-done.42, f32[8,2048]{1,0:T(8,128)} %fusion.50.refs_3_), custom_call_target="tpu_custom_call" | custom-call | flops 149999992832 | bytes 20971520 | tf_op jit(solution)/shard_map/down_sum/pallas_call | solution.py:207
  842.2 0.7 fusion.173
  842.9 1.4 fusion.123
  844.4 7.3 bitcast_select_fusion.1
  851.7 7.6 maximum_bitcast_fusion
  859.3 3.3 fusion.87
  862.6 4.2 copy.110
  866.8 2.5 copy.111
  869.4 4.8 copy.192
  (141 shorter events, 6.4 us)
Async XLA Ops:
  7.2 256.4 %all-gather.5.cloned.1.call-start = ((), (), s32[]{:S(2)}) async-start(), calls=%async_computation.2 | async-start | bytes 8650752 | tf_op jit(solution)/shard_map/all_gather | solution.py:338
  9.1 581.8 %all-gather.7.cloned.1.call-start = ((), (), s32[]{:S(2)}) async-start(), calls=%async_computation.3 | async-start | bytes 8650752 | tf_op jit(solution)/shard_map/all_gather | solution.py:338
  31.7 4.3 copy-start.32
  31.7 5.0 copy-start.6
  36.0 12.3 %copy-start.9 = (f32[1024,64]{0,1:T(8,128)}, f32[1024,64]{0,1:T(8,128)S(1)}, u32[]{:S(2)}) copy-start(f32[1024,64]{0,1:T(8,128)S(1)} %get-tuple-element.108) | copy-start | bytes 786436
  36.0 12.3 %copy-start.11 = (f32[1024,64]{0,1:T(8,128)}, f32[1024,64]{0,1:T(8,128)S(1)}, u32[]{:S(2)}) copy-start(f32[1024,64]{0,1:T(8,128)S(1)} %get-tuple-element.109) | copy-start | bytes 786436
  45.8 2.6 copy-start.4
  48.3 5.0 copy-start.41
  48.3 5.7 copy-start.33
  50.2 205.6 %collective-permute-start = (bf16[2,1024,4,128]{1,3,2,0:T(8,128)(2,1)S(1)}, bf16[2,1024,4,128]{1,3,2,0:T(8,128)(2,1)}, u32[]{:S(2)}, u32[]{:S(2)}) collective-permute-start(bf16[2,1024,4,128]{1,3,2,0:T(8,128)(2,1)S(1)} %pad_maximum_fusion.1), channel_id=1, source_target_pairs={{0,2},{1,3},{2,0},{3,1},{4,6},{5,7},{6,4},{7,5},{8,10},{9,11},{10,... | collective-permute-start | bytes 6291464 | tf_op jit(solution)/shard_map/ppermute | solution.py:312
  54.0 16.6 %copy-start.23 = (pred[8,256]{1,0:T(8,128)(4,1)}, pred[8,256]{1,0:T(8,128)(4,1)S(1)}, u32[]{:S(2)}) copy-start(pred[8,256]{1,0:T(8,128)(4,1)S(1)} %get-tuple-element.115) | copy-start | bytes 6148
  54.6 10.1 %copy-start.15 = (bf16[8,2048]{1,0:T(8,128)(2,1)S(1)}, bf16[8,2048]{1,0:T(8,128)(2,1)}, u32[]{:S(2)}) copy-start(bf16[8,2048]{1,0:T(8,128)(2,1)} %param.23) | copy-start | bytes 98308
  64.7 2.2 copy-start.2
  65.9 3.4 copy-start.25
  66.0 3.4 copy-start.27
  66.9 3.8 copy-start
  258.9 379.1 %all-to-all-start = ((bf16[2,1024,4,128]{1,3,0,2:T(8,128)(2,1)}), bf16[2,1024,4,128]{1,3,0,2:T(8,128)(2,1)}, u32[]{:S(2)}, u32[]{:S(2)}) async-start(bf16[2,1024,4,128]{1,3,0,2:T(8,128)(2,1)} %copy.104), calls=%async_computation | async-start | bytes 4194304 | tf_op jit(solution)/shard_map/all_to_all | solution.py:313
  263.6 13.5 %copy-start.40 = (f32[1,1,2048]{2,1,0:T(1,128)S(1)}, f32[1,1,2048]{2,1,0:T(1,128)}, u32[]{:S(2)}) copy-start(f32[1,1,2048]{2,1,0:T(1,128)} %get-tuple-element.89) | copy-start | bytes 24580
  277.0 17.4 %copy-start.43 = (bf16[1024,2048]{1,0:T(8,128)(2,1)}, bf16[1024,2048]{1,0:T(8,128)(2,1)S(1)}, u32[]{:S(2)}) copy-start(bf16[1024,2048]{1,0:T(8,128)(2,1)S(1)} %get-tuple-element.119.refs_2_) | copy-start | bytes 12582916
  470.7 3.5 copy-start.8
  470.7 3.4 copy-start.39
  483.4 2.7 copy-start.5
  483.6 2.5 copy-start.10
  483.6 2.5 copy-start.12
  486.1 2.9 copy-start.14
  488.4 146.5 %collective-permute-start.1 = (bf16[2,1024,4,128]{1,3,2,0:T(8,128)(2,1)}, bf16[2,1024,4,128]{1,3,2,0:T(8,128)(2,1)}, u32[]{:S(2)}, u32[]{:S(2)}) collective-permute-start(bf16[2,1024,4,128]{1,3,2,0:T(8,128)(2,1)} %pad_maximum_fusion.2), channel_id=1, source_target_pairs={{0,2},{1,3},{2,0},{3,1},{4,6},{5,7},{6,4},{7,5},{8,10},{9,11},{10,... | collective-permute-start | bytes 6291464 | tf_op jit(solution)/shard_map/ppermute | solution.py:312
  499.1 9.1 %copy-start.16 = (bf16[8,2048]{1,0:T(8,128)(2,1)S(1)}, bf16[8,2048]{1,0:T(8,128)(2,1)}, u32[]{:S(2)}) copy-start(bf16[8,2048]{1,0:T(8,128)(2,1)} %param.23) | copy-start | bytes 98308
  499.1 9.1 %copy-start.19 = (bf16[8,2048]{1,0:T(8,128)(2,1)S(1)}, bf16[8,2048]{1,0:T(8,128)(2,1)}, u32[]{:S(2)}) copy-start(bf16[8,2048]{1,0:T(8,128)(2,1)} %get-tuple-element.15) | copy-start | bytes 98308
  499.1 9.1 %copy-start.35 = (bf16[8,2048]{1,0:T(8,128)(2,1)S(1)}, bf16[8,2048]{1,0:T(8,128)(2,1)}, u32[]{:S(2)}) copy-start(bf16[8,2048]{1,0:T(8,128)(2,1)} %get-tuple-element.17) | copy-start | bytes 98308
  499.1 9.3 %copy-start.31 = (f32[1,1,2048]{2,1,0:T(1,128)S(1)}, f32[1,1,2048]{2,1,0:T(1,128)}, u32[]{:S(2)}) copy-start(f32[1,1,2048]{2,1,0:T(1,128)} %get-tuple-element.87) | copy-start | bytes 24580
  506.9 5.5 copy-start.26
  506.9 5.5 copy-start.28
  506.9 6.3 copy-start.3
  508.4 113.7 %copy-start.17 = (bf16[8,2048]{1,0:T(8,128)(2,1)}, bf16[8,2048]{1,0:T(8,128)(2,1)S(1)}, u32[]{:S(2)}) copy-start(bf16[8,2048]{1,0:T(8,128)(2,1)S(1)} %get-tuple-element.43) | copy-start | bytes 98308
  508.4 5.4 copy-start.24
  508.4 5.8 copy-start.13
  508.4 6.2 copy-start.7
  512.3 2.3 copy-start.22
  590.9 13.5 %copy-start.38 = (f32[1,1,2048]{2,1,0:T(1,128)S(1)}, f32[1,1,2048]{2,1,0:T(1,128)}, u32[]{:S(2)}) copy-start(f32[1,1,2048]{2,1,0:T(1,128)} %get-tuple-element.88) | copy-start | bytes 24580
  604.3 17.6 %copy-start.42 = (bf16[1024,2048]{1,0:T(8,128)(2,1)}, bf16[1024,2048]{1,0:T(8,128)(2,1)S(1)}, u32[]{:S(2)}) copy-start(bf16[1024,2048]{1,0:T(8,128)(2,1)S(1)} %get-tuple-element.123.refs_2_) | copy-start | bytes 12582916
  604.4 17.6 %copy-start.20 = (bf16[8,2048]{1,0:T(8,128)(2,1)S(1)}, bf16[8,2048]{1,0:T(8,128)(2,1)}, u32[]{:S(2)}) copy-start(bf16[8,2048]{1,0:T(8,128)(2,1)} %get-tuple-element.19) | copy-start | bytes 98308
  604.4 17.7 %copy-start.36 = (f32[1,1,2048]{2,1,0:T(1,128)S(1)}, f32[1,1,2048]{2,1,0:T(1,128)}, u32[]{:S(2)}) copy-start(f32[1,1,2048]{2,1,0:T(1,128)} %get-tuple-element.84) | copy-start | bytes 24580
  638.0 221.2 %all-to-all-start.1 = ((bf16[2,1024,4,128]{1,3,0,2:T(8,128)(2,1)}), bf16[2,1024,4,128]{1,3,0,2:T(8,128)(2,1)}, u32[]{:S(2)}, u32[]{:S(2)}) async-start(bf16[2,1024,4,128]{1,3,0,2:T(8,128)(2,1)} %copy.105), calls=%async_computation.1 | async-start | bytes 4194304 | tf_op jit(solution)/shard_map/all_to_all | solution.py:313
  642.5 199.7 %copy-start.34 = (bf16[8,4,128]{2,0,1:T(8,128)(2,1)S(1)}, bf16[8,4,128]{2,0,1:T(8,128)(2,1)}, u32[]{:S(2)}) copy-start(bf16[8,4,128]{2,0,1:T(8,128)(2,1)} %get-tuple-element.41) | copy-start | bytes 24580
  642.5 200.4 %copy-start.18 = (bf16[8,2048]{1,0:T(8,128)(2,1)S(1)}, bf16[8,2048]{1,0:T(8,128)(2,1)}, u32[]{:S(2)}) copy-start(bf16[8,2048]{1,0:T(8,128)(2,1)} %copy-done.17) | copy-start | bytes 98308
  642.5 200.4 %copy-start.21 = (bf16[8,2048]{1,0:T(8,128)(2,1)S(1)}, bf16[8,2048]{1,0:T(8,128)(2,1)}, u32[]{:S(2)}) copy-start(bf16[8,2048]{1,0:T(8,128)(2,1)} %get-tuple-element.19) | copy-start | bytes 98308
  642.5 201.8 %copy-start.1 = (bf16[2,8,256,4,1,128]{5,3,4,2,1,0:T(4,128)(2,1)S(1)}, bf16[2,8,256,4,1,128]{5,3,4,2,1,0:T(4,128)(2,1)}, u32[]{:S(2)}) copy-start(bf16[2,8,256,4,1,128]{5,3,4,2,1,0:T(4,128)(2,1)} %param.25) | copy-start | bytes 12582916
  642.5 201.8 %copy-start.29 = (bf16[8,4,128]{2,1,0:T(4,128)(2,1)S(1)}, bf16[8,4,128]{2,1,0:T(4,128)(2,1)}, u32[]{:S(2)}) copy-start(bf16[8,4,128]{2,1,0:T(4,128)(2,1)} %copy.106) | copy-start | bytes 24580
  642.5 201.8 %copy-start.30 = (bf16[8,4,128]{2,1,0:T(4,128)(2,1)S(1)}, bf16[8,4,128]{2,1,0:T(4,128)(2,1)}, u32[]{:S(2)}) copy-start(bf16[8,4,128]{2,1,0:T(4,128)(2,1)} %copy.108) | copy-start | bytes 24580
  642.6 201.8 %copy-start.37 = (pred[8,256]{1,0:T(8,128)(4,1)S(1)}, pred[8,256]{1,0:T(8,128)(4,1)}, u32[]{:S(2)}) copy-start(pred[8,256]{1,0:T(8,128)(4,1)} %get-tuple-element.114) | copy-start | bytes 6148
Sparse Core Ops, SparseCore 0:
  10.8 94.8 all-gather.4
  108.6 90.1 all-gather.6

commit v2 on v1

--- a/solution.py
+++ b/solution.py
@@ -12,6 +12,8 @@
 SUM_ROWS = 32
 DOT_ROWS = 128
 DOT_COLS = 512
+FF_COLS = 256
+SUM_VMEM_BYTES = 63 * 1024 * 1024
 VMEM_BYTES = 56 * 1024 * 1024
 MESH = pl.DeviceIdType.MESH
 
@@ -115,29 +117,109 @@
     )(ctx, small_part)
 
 
-def sum_kernel(tp_size, act_ref, wd_ref, hid_ref, part_ref, out_ref, small_ref, total, came, held, up_send, up_recv, dn_send, dn_recv, gu_send, gu_recv, gd_send, gd_recv, sm_send, sm_recv):
+def sum_kernel(layer, tp_size, ctx_hbm, hid_hbm, wo_hbm, gu_hbm, wd_hbm, gain_ref, part_ref, out_ref, small_ref, ctx_ref, hid_ref, wo_ref, gu_ref, wd_ref, norm_ref, act_ref, total, came, held, in_sems, up_send, up_recv, dn_send, dn_recv, gu_send, gu_recv, gd_send, gd_recv, sm_send, sm_recv):
     me = lax.axis_index('tp')
     last = tp_size - 1
     half = hid_ref.shape[0] // 2
     chunks = half // SUM_ROWS
     per_dot = DOT_ROWS // SUM_ROWS
     width = hid_ref.shape[1]
+    ff_loc = wd_ref.shape[0]
+    shard = ctx_ref.shape[2]
+    loads = [
+        pltpu.make_async_copy(ctx_hbm, ctx_ref, in_sems.at[0]),
+        pltpu.make_async_copy(hid_hbm, hid_ref, in_sems.at[1]),
+        pltpu.make_async_copy(wo_hbm, wo_ref, in_sems.at[2]),
+        pltpu.make_async_copy(gu_hbm.at[layer], gu_ref, in_sems.at[3]),
+        pltpu.make_async_copy(wd_hbm.at[layer], wd_ref, in_sems.at[4]),
+    ]
+    for load in loads:
+        load.start()
     greet(me, tp_size)
     share_small(me, tp_size, part_ref, held, sm_send, sm_recv)
     streams = ((1, half, up_send, up_recv, gu_send, gu_recv), (-1, 0, dn_send, dn_recv, gd_send, gd_recv))
-
-    def tick(step, carry):
-        @pl.when((lax.rem(step, per_dot) == 0) & (step < chunks))
-        def _():
-            for base in (half, 0):
-                rows = pl.ds(pl.multiple_of(base + step * SUM_ROWS, SUM_ROWS), DOT_ROWS)
-
-                def columns(idx, inner):
-                    cols = pl.ds(pl.multiple_of(idx * DOT_COLS, DOT_COLS), DOT_COLS)
-                    total[rows, cols] = jnp.dot(act_ref[rows, :], wd_ref[:, cols], preferred_element_type=jnp.float32)
-                    return inner
-
-                lax.fori_loop(0, width // DOT_COLS, columns, 0)
+    full_ff = ff_loc // FF_COLS
+    rest = ff_loc - full_ff * FF_COLS
+    first_part = (full_ff + 1) // 2
+
+    def activate(start, size):
+        normed = norm_ref[...]
+        contract = (((1,), (1,)), ((), ()))
+        gate = lax.dot_general(normed, gu_ref[0, pl.ds(start, size), :], contract, preferred_element_type=jnp.float32)
+        up = lax.dot_general(normed, gu_ref[1, pl.ds(start, size), :], contract, preferred_element_type=jnp.float32)
+        gate = gate.astype(jnp.bfloat16).astype(jnp.float32)
+        up = up.astype(jnp.bfloat16).astype(jnp.float32)
+        act_ref[:, pl.ds(start, size)] = (jax.nn.silu(gate) * up).astype(jnp.bfloat16)
+
+    def tick(time, carry):
+        step = time - per_dot
+        stage = lax.rem(time, per_dot)
+        block = time // per_dot
+        working = time < chunks
+        block_rows = [pl.ds(pl.multiple_of(base + block * DOT_ROWS, DOT_ROWS), DOT_ROWS) for base in (half, 0)]
+
+        @pl.when(time == 0)
+        def _():
+            for load in loads[:3]:
+                load.wait()
+
+        @pl.when(time == 1)
+        def _():
+            loads[3].wait()
+
+        @pl.when(time == 3)
+        def _():
+            loads[4].wait()
+
+        @pl.when(working & (stage == 0))
+        def _():
+            def columns(idx, inner):
+                cols = pl.ds(pl.multiple_of(idx * DOT_COLS, DOT_COLS), DOT_COLS)
+                attn = None
+                for src in range(tp_size):
+                    both = jnp.concatenate([ctx_ref[src, rows, :] for rows in block_rows], axis=0)
+                    term = jnp.dot(both, wo_ref[src * shard:(src + 1) * shard, cols], preferred_element_type=jnp.float32)
+                    attn = term if attn is None else attn + term
+                attn = attn.astype(jnp.bfloat16).astype(jnp.float32)
+                for idx_rows, rows in enumerate(block_rows):
+                    old = hid_ref[rows, cols].astype(jnp.float32)
+                    hid_ref[rows, cols] = (old + attn[idx_rows * DOT_ROWS:(idx_rows + 1) * DOT_ROWS]).astype(jnp.bfloat16)
+                return inner
+
+            lax.fori_loop(0, width // DOT_COLS, columns, 0)
+            for idx_rows, rows in enumerate(block_rows):
+                for sub in range(0, DOT_ROWS, 32):
+                    piece = pl.ds(pl.multiple_of(rows.start + sub, 32), 32)
+                    hid = hid_ref[piece, :].astype(jnp.float32)
+                    inv_rms = lax.rsqrt(jnp.mean(hid * hid, axis=-1, keepdims=True) + EPSILON)
+                    norm_ref[idx_rows * DOT_ROWS + sub:idx_rows * DOT_ROWS + sub + 32, :] = (hid * inv_rms * gain_ref[...]).astype(jnp.bfloat16)
+
+        @pl.when(working & ((stage == 1) | (stage == 2)))
+        def _():
+            low = (stage - 1) * first_part
+            high = first_part + (stage - 1) * (full_ff - first_part)
+
+            def features(idx, inner):
+                activate(pl.multiple_of(idx * FF_COLS, FF_COLS), FF_COLS)
+                return inner
+
+            lax.fori_loop(low, high, features, 0)
+
+        if rest:
+            @pl.when(working & (stage == 2))
+            def _():
+                activate(full_ff * FF_COLS, rest)
+
+        @pl.when(working & (stage == 3))
+        def _():
+            def columns(idx, inner):
+                cols = pl.ds(pl.multiple_of(idx * DOT_COLS, DOT_COLS), DOT_COLS)
+                part = jnp.dot(act_ref[...], wd_ref[:, cols], preferred_element_type=jnp.float32)
+                for idx_rows, rows in enumerate(block_rows):
+                    total[rows, cols] = part[idx_rows * DOT_ROWS:(idx_rows + 1) * DOT_ROWS]
+                return inner
+
+            lax.fori_loop(0, width // DOT_COLS, columns, 0)
 
         for sign, base, send, recv, g_send, g_recv in streams:
             place = me if sign == 1 else last - me
@@ -180,7 +262,7 @@
                     to_peer(out_ref.at[rows], out_ref.at[rows], g_send.at[chunk], g_recv.at[chunk], prev).start()
         return carry
 
-    lax.fori_loop(0, chunks + 2 * last, tick, 0)
+    lax.fori_loop(0, per_dot + chunks + 2 * last, tick, 0)
 
     def drain(chunk, carry):
         for sign, base, send, recv, g_send, g_recv in streams:
@@ -200,20 +282,35 @@
     sum_small(me, tp_size, part_ref, held, sm_send, sm_recv, small_ref)
 
 
-def down_and_sum(act, w_down, hidden, small_part, tp_size):
+def mlp_and_sum(layer, ctx_full, hidden, wo_full, w_gu, w_down, gain, small_part, tp_size):
     rows, width = hidden.shape
     chunks = rows // 2 // SUM_ROWS
+    ff_loc = w_down.shape[1]
     vmem = pl.BlockSpec(memory_space=pltpu.VMEM)
+    hbm = pl.BlockSpec(memory_space=pl.ANY)
+    bf16 = jnp.bfloat16
     return pl.pallas_call(
-        lambda *refs: sum_kernel(tp_size, *refs),
-        out_shape=(jax.ShapeDtypeStruct(hidden.shape, hidden.dtype), jax.ShapeDtypeStruct(small_part.shape, jnp.bfloat16)),
-        in_specs=[vmem] * 4,
+        lambda *refs: sum_kernel(layer, tp_size, *refs),
+        out_shape=(jax.ShapeDtypeStruct(hidden.shape, hidden.dtype), jax.ShapeDtypeStruct(small_part.shape, bf16)),
+        in_specs=[hbm] * 5 + [vmem] * 2,
         out_specs=(vmem, vmem),
-        scratch_shapes=[pltpu.VMEM((rows, width), jnp.float32), pltpu.VMEM((rows, width), jnp.float32), pltpu.VMEM((tp_size,) + small_part.shape, jnp.float32)] + [pltpu.SemaphoreType.DMA((chunks,))] * 8 + [pltpu.SemaphoreType.DMA((tp_size - 1,)), pltpu.SemaphoreType.DMA((tp_size,))],
-        compiler_params=pltpu.CompilerParams(collective_id=1, has_side_effects=True, vmem_limit_bytes=VMEM_BYTES),
-        cost_estimate=pl.CostEstimate(flops=150_000_000_000, bytes_accessed=rows * width * 10, transcendentals=0),
-        name='down_sum',
-    )(act, w_down, hidden, small_part)
+        scratch_shapes=[
+            pltpu.VMEM(ctx_full.shape, bf16),
+            pltpu.VMEM((rows, width), bf16),
+            pltpu.VMEM(wo_full.shape, bf16),
+            pltpu.VMEM((2, ff_loc, width), bf16),
+            pltpu.VMEM((ff_loc, width), bf16),
+            pltpu.VMEM((2 * DOT_ROWS, width), bf16),
+            pltpu.VMEM((2 * DOT_ROWS, ff_loc), bf16),
+            pltpu.VMEM((rows, width), jnp.float32),
+            pltpu.VMEM((rows, width), jnp.float32),
+            pltpu.VMEM((tp_size,) + small_part.shape, jnp.float32),
+            pltpu.SemaphoreType.DMA((5,)),
+        ] + [pltpu.SemaphoreType.DMA((chunks,))] * 8 + [pltpu.SemaphoreType.DMA((tp_size - 1,)), pltpu.SemaphoreType.DMA((tp_size,))],
+        compiler_params=pltpu.CompilerParams(collective_id=1 + layer, has_side_effects=True, vmem_limit_bytes=SUM_VMEM_BYTES),
+        cost_estimate=pl.CostEstimate(flops=160_000_000_000, bytes_accessed=rows * width * 20, transcendentals=0),
+        name='mlp_sum',
+    )(ctx_full, hidden, wo_full, w_gu, w_down, gain, small_part)
 
 
 def rms_norm(hidden, gain_vec):
@@ -273,7 +370,7 @@
     return context.astype(jnp.bfloat16)
 
 
-def run_layers(prompt, s_valid, w_qkv_pre, wo_full, w_gu_pre, w_down_pre, gains_pre, tokens, k_cache, v_cache, c_len, w_qkv_dec, w_out_dec, w_gu_dec, w_down_dec, gains_dec, partner_perm, tp_size):
+def run_layers(prompt, s_valid, w_qkv_pre, wo_parts, w_gu_pre, w_down_pre, gains_pre, tokens, k_cache, v_cache, c_len, w_qkv_dec, w_out_dec, w_gu_dec, w_down_dec, gains_dec, partner_perm, tp_size):
     layers, row_count, cache_len, heads_loc, _, head_dim = k_cache.shape
     width = tokens.shape[1]
     seq_len = prompt.shape[0]
@@ -288,11 +385,12 @@
     positions = jnp.arange(seq_len)
     cos_pre, sin_pre = rope_tables(positions, head_dim)
     allowed = (positions[None, :] <= positions[:, None]) & (positions[None, :] < s_valid[:, None])
+    wqkv_flat = w_qkv_pre.reshape(layers, width, -1)
     hidden = prompt
     installed, k_next, v_next = [], [], []
     for layer_idx in range(layers):
         normed = rms_norm(hidden, gains_pre[layer_idx, 0])
-        qkv_out = jnp.einsum('sd,dkhe->skhe', normed, w_qkv_pre[layer_idx], preferred_element_type=jnp.float32)
+        qkv_out = jnp.dot(normed, wqkv_flat[layer_idx], preferred_element_type=jnp.float32).reshape(seq_len, 3, heads_loc, head_dim)
         queries = apply_rope(qkv_out[:, 0], cos_pre, sin_pre).astype(jnp.bfloat16)
         keys_new = apply_rope(qkv_out[:, 1], cos_pre, sin_pre).astype(jnp.bfloat16)
         values_new = qkv_out[:, 2].astype(jnp.bfloat16)
@@ -309,35 +407,36 @@
         v_next.append(jnp.where(write_at, v_tok[:, None], v_local[layer_idx]))
 
         ctx_full, attn_tok = gather_ctx(context, part_tok, tp_size)
-        kv_new = lax.ppermute(jnp.stack([keys_new, values_new]), 'side', partner_perm)
-        installed.append(lax.all_to_all(kv_new, 'tp', 2, 2, tiled=True))
-
-        attn = jnp.einsum('zsf,zfd->sd', ctx_full, wo_full[layer_idx], preferred_element_type=jnp.float32)
-        hidden = add_residual(hidden, attn.astype(jnp.bfloat16))
-        act = swiglu(hidden, gains_pre[layer_idx, 1], w_gu_pre[layer_idx])
+        kv_new = lax.all_to_all(jnp.stack([keys_new, values_new]), 'tp', 2, 2, tiled=True)
+        installed.append(lax.ppermute(kv_new, 'side', partner_perm))
+
+        if layer_idx == 0:
+            wo_full = gather_wo(wo_parts[0])
+        else:
+            wo_full = gather_wo(wo_next)
         tokens = add_residual(tokens, attn_tok)
         act_tok = swiglu(tokens, gains_dec[layer_idx, 1], w_gu_dec[layer_idx])
         mlp_tok = jnp.einsum('bf,fd->bd', act_tok, w_down_dec[layer_idx], preferred_element_type=jnp.float32)
-        hidden, down_tok = down_and_sum(act, w_down_pre[layer_idx], hidden, mlp_tok, tp_size)
+        hidden, down_tok = mlp_and_sum(layer_idx, ctx_full, hidden, wo_full, w_gu_pre, w_down_pre, gains_pre[layer_idx, 1][None], mlp_tok, tp_size)
+        if layer_idx + 1 < layers:
+            wo_next, down_tok = lax.optimization_barrier((wo_parts[layer_idx + 1], down_tok))
         tokens = add_residual(tokens, down_tok)
     k_new = jnp.stack(k_next).reshape(k_cache.shape)
     v_new = jnp.stack(v_next).reshape(v_cache.shape)
     return hidden, tokens, installed, k_new, v_new
 
 
-def gather_wo(w_out, side_size, pair_size):
+def parts_of_wo(w_out, side_size, pair_size):
     layers, heads_loc, head_dim, width = w_out.shape
     rows = heads_loc * head_dim
-    copies = side_size * pair_size
-    part = rows // copies
+    part = rows // (side_size * pair_size)
     place = lax.axis_index('pair') * side_size + lax.axis_index('side')
     flat = w_out.reshape(layers, rows, width)
-    mine = lax.dynamic_slice_in_dim(flat, place * part, part, axis=1)
-    full = []
-    for layer_idx in range(layers):
-        everything = lax.all_gather(mine[layer_idx], ('tp', 'pair', 'side'), axis=0, tiled=True)
-        full.append(everything.reshape(-1, rows, width))
-    return full
+    return [lax.dynamic_slice(flat, (layer_idx, place * part, 0), (1, part, width))[0] for layer_idx in range(layers)]
+
+
+def gather_wo(part):
+    return lax.all_gather(part, ('tp', 'pair', 'side'), axis=0, tiled=True)
 
 
 def solution(mesh):
@@ -354,8 +453,8 @@
     out_specs = (rows_spec, rows_spec, prompt_spec, prompt_spec, cache_spec, cache_spec)
 
     def device_fn(prompt_x, s_len, w_qkv_pre, w_out_pre, w_gu_pre, w_down_pre, gain_pre, dec_tokens, k_cache, v_cache, c_len, w_qkv_dec, w_out_dec, w_gu_dec, w_down_dec, gain_dec):
-        wo_full = gather_wo(w_out_pre, side_size, pair_size)
-        hidden, dec_out, installed, k_cache_new, v_cache_new = run_layers(prompt_x, s_len, w_qkv_pre, wo_full, w_gu_pre, w_down_pre, gain_pre, dec_tokens, k_cache, v_cache, c_len, w_qkv_dec, w_out_dec, w_gu_dec, w_down_dec, gain_dec, partner_perm, tp_size)
+        wo_parts = parts_of_wo(w_out_pre, side_size, pair_size)
+        hidden, dec_out, installed, k_cache_new, v_cache_new = run_layers(prompt_x, s_len, w_qkv_pre, wo_parts, w_gu_pre, w_down_pre, gain_pre, dec_tokens, k_cache, v_cache, c_len, w_qkv_dec, w_out_dec, w_gu_dec, w_down_dec, gain_dec, partner_perm, tp_size)
         prompt_kv = jnp.stack(installed, axis=1)[:, :, :, :, None, :]
         return hidden, dec_out, prompt_kv[0], prompt_kv[1], k_cache_new, v_cache_new
 

time: 891 us -> 841 us (0.944)
  matrix products: 151 us -> 85 us
  waiting for transfers between devices: 0.08 us -> 22.8 us
  Pallas kernels: 568 us -> 583 us
  local copies, waits for them, and re-layouts: 91.4 us -> 78.7 us
    dot_general x4 -> x2, matrix products: 48 us -> 13.3 us  [swiglu(): jnp.einsum('sd,kfd->skf', normed, w_gu, preferred_element_type=jnp.float32)]
    pallas_call x2, Pallas kernels: 195 us -> 227 us  [gather_ctx(): pl.pallas_call(lambda *refs: ctx_kernel(tp_size, *refs), out_shape=(jax.S...]
    ppermute x2, waiting for transfers between devices: 0.01 us -> 22.1 us  [run_layers(): installed.append(lax.ppermute(kv_new, 'side', partner_perm))]
    unnamed x93 -> x91, local copies, waits for them, and re-layouts: 38.4 us -> 17.1 us
    unnamed x2 -> x0, matrix products: 18.3 us -> none
    pallas_call x2, Pallas kernels: 373 us -> 357 us  [mlp_and_sum(): pl.pallas_call(lambda *refs: sum_kernel(layer, tp_size, *refs), out_shape...]
    squeeze x1 -> x3, local copies, waits for them, and re-layouts: 10.8 us -> 23.2 us  [the longest x2 21.3 us: run_layers(): wqkv_flat[layer_idx]]
  transfers between devices with their start and end apart: 6 -> 6, of which waited for: 0 -> 1; matrix products, arithmetic and copies ran while one was open for 30% -> 22% of each run, Pallas kernels for 64% -> 49%
where the time goes in v2:
time: 841 us; the launch traced here: 833 us
  Pallas kernels  583 us (69%)
  matrix products  85 us (10%)
  local copies, waits for them, and re-layouts  78.7 us (9%)
  other arithmetic  34.9 us (4%)
  waiting for transfers between devices  22.8 us (3%)
  between operations  15.5 us (2%)
  starting transfers between devices  13.2 us (2%)
    pallas_call x2, Pallas kernels, mlp_and_sum(): pl.pallas_call(lambda *refs: sum_kernel(layer, tp_size, *refs), out_shape...  357 us
    pallas_call x2, Pallas kernels, gather_ctx(): pl.pallas_call(lambda *refs: ctx_kernel(tp_size, *refs), out_shape=(jax.S...  227 us
    ppermute x2, waiting for transfers between devices, run_layers(): installed.append(lax.ppermute(kv_new, 'side', partner_perm))  22.1 us
    squeeze x2, local copies, waits for them, and re-layouts, run_layers(): wqkv_flat[layer_idx]  21.3 us
    sub x2, matrix products, prompt_attention(): prob_bf = jax.nn.softmax(scores, axis=-1).astype(jnp.bfloat16)  20.7 us
    dot_general x2, matrix products, run_layers(): jnp.dot(normed, wqkv_flat[layer_idx], preferred_element_type=jnp.float32)  18.1 us
    unnamed x91, local copies, waits for them, and re-layouts  17.1 us
  transfers between devices with their start and end apart: 6, of which 1 were waited for; matrix products, arithmetic and copies ran while one was open for 22% of the time, Pallas kernels for 49%

profile of v2, /device:TPU:0, one launch (start us, length us, event | category | flops | bytes accessed | tf_op | source)
XLA Modules:
  0.0 833.2 jit_solution(15305248051044892165)
XLA Ops:
  7.2 1.9 dynamic-slice_bitcast_fusion
  9.2 1.4 slice_bitcast_fusion.16
  10.6 12.0 %fusion.166 = (bf16[1,2048,3,4,128]{4,3,2,1,0:T(4,128)(2,1)}, bf16[1,2048,3,4,128]{4,3,2,1,0:T(4,128)(2,1)}) fusion(bf16[2,2048,3,4,128]{4,3,2,1,0:T(4,128)(2,1)} %param.18), kind=kLoop, calls=%fused_computation.262 | loop fusion | bytes 25165824 | tf_op jit(solution)/shard_map/slice | solution.py:393
  22.5 10.6 %copy.134 = bf16[1,2048,3,4,128]{1,4,3,2,0:T(8,128)(2,1)} copy(bf16[1,2048,3,4,128]{4,3,2,1,0:T(4,128)(2,1)} %get-tuple-element.52) | data formatting | bytes 12582912 | tf_op jit(solution)/shard_map/squeeze | solution.py:393
  33.2 3.2 fusion.10
  36.6 9.1 %fusion.28 = f32[1024,3,4,128]{0,3,2,1:T(8,128)S(1)} fusion(bf16[1,2048,3,4,128]{1,4,3,2,0:T(8,128)(2,1)} %copy.134, bf16[1024,2048]{1,0:T(8,128)(2,1)S(1)} %copy-done.6, f32[2048]{0:T(1024)S(1)} %bitcast.233, f32[1024]{0:T(1024)S(1)} %add_rsqrt_fusion.1), kind=kOutput, calls=%fused_computation.40 | convolution fusion | flops 6450839552 | bytes 16789504 | tf_op jit(solution)/shard_map/dot_general | solution.py:393
  45.7 0.3 slice_bitcast_fusion.7
  46.0 2.4 copy-done.5
  48.6 1.0 multiply_cosine_fusion
  49.6 0.7 subtract_convert_fusion.3
  50.5 1.6 copy.98
  52.1 6.6 all-to-all-start
  59.3 0.4 fusion.44
  59.7 10.2 %fusion.168 = (f32[4,1024]{1,0:T(4,128)S(1)}, f32[4,1024,1024]{1,2,0:T(8,128)}) fusion(pred[1024,1024]{0,1:T(8,128)(4,1)S(1)} %fusion.44, bf16[1024,4,64]{0,2,1:T(8,128)(2,1)S(1)} %get-tuple-element.80, bf16[1024,4,64]{0,2,1:T(8,128)(2,1)S(1)} %get-tuple-element.81, bf16[1024,4,64]{0,2,1:T(8,128)(2,1)S(1)} %get-tuple-element.75, ...), kind=kOutput, calls=%fused_computation.264 | convolution fusion | flops 1094714368 | bytes 19939328 | tf_op jit(solution)/shard_map/sub | solution.py:354
  69.9 7.7 fusion.67
  77.6 1.3 copy.135.refs_0_
  79.2 0.6 fusion.167
  79.9 10.1 %fusion.165 = (bf16[1,2048,3,4,1,128]{5,3,4,2,1,0:T(4,128)(2,1)}, bf16[1,2048,3,4,1,128]{5,3,4,2,1,0:T(4,128)(2,1)S(1)}) fusion(bf16[2,2048,3,4,1,128]{5,3,4,2,1,0:T(4,128)(2,1)} %param.27), kind=kLoop, calls=%fused_computation.261 | loop fusion | bytes 25165824 | tf_op jit(solution)/shard_map/slice | solution.py:400
  90.0 1.0 fusion.25
  91.3 0.7 iota_compare_fusion.1
  91.9 0.2 copy-done.2
  92.2 2.4 slice_bitcast_fusion.9
  94.6 0.6 fusion.60
  95.6 2.5 slice_bitcast_fusion.8
  98.1 0.4 fusion.58
  98.5 1.1 convolution_bitcast_fusion.1.refs_1_
  99.6 103.5 %ctx_gather.2 = (bf16[4,1024,512]{2,1,0:T(8,128)(2,1)}, bf16[8,2048]{1,0:T(8,128)(2,1)}) custom-call(bf16[1024,512]{1,0:T(8,128)(2,1)} %copy.135.refs_0_, f32[8,2048]{1,0:T(8,128)} %convolution_bitcast_fusion.1.refs_1_), custom_call_target="tpu_custom_call" | custom-call | flops 70000001024 | bytes 5242880 | tf_op jit(solution)/shard_map/ctx_gather/pallas_call | solution.py:108
  203.1 0.6 copy.100
  203.7 0.6 copy.102
  204.3 10.6 %copy.137 = bf16[1,2048,3,4,128]{1,4,3,2,0:T(8,128)(2,1)} copy(bf16[1,2048,3,4,128]{4,3,2,1,0:T(4,128)(2,1)} %get-tuple-element.53) | data formatting | bytes 12582912 | tf_op jit(solution)/shard_map/squeeze | solution.py:393
  215.1 6.1 fusion.45
  221.2 4.1 fusion.32.refs_6_
  225.2 1.5 collective-permute-start
  226.8 179.7 %mlp_sum.2 = (bf16[1024,2048]{1,0:T(8,128)(2,1)}, bf16[8,2048]{1,0:T(8,128)(2,1)}) custom-call(bf16[4,1024,512]{2,1,0:T(8,128)(2,1)} %get-tuple-element.16.refs_0_, bf16[1024,2048]{1,0:T(8,128)(2,1)} %refs_1_.1, bf16[2048,2048]{1,0:T(8,128)(2,1)} %bitcast.234, bf16[2,2,1376,2048]{3,2,1,0:T(8,128)(2,1)} %refs_3_.3, bf16[2,1376,2048]{2,1,0:T(8,128)(2,1)} %refs_4_.3, ...), custom_call_target="tpu_custom_call" | custom-call | flops 160000000000 | bytes 41943040 | tf_op jit(solution)/shard_map/mlp_sum/pallas_call | solution.py:292
  406.5 3.2 fusion.13
  409.9 9.0 %fusion.26 = f32[1024,3,4,128]{0,3,2,1:T(8,128)S(1)} fusion(bf16[1,2048,3,4,128]{1,4,3,2,0:T(8,128)(2,1)} %copy.137, bf16[1024,2048]{1,0:T(8,128)(2,1)S(1)} %copy-done.9, f32[2048]{0:T(1024)S(1)} %bitcast.232, f32[1024]{0:T(1024)S(1)} %add_rsqrt_fusion), kind=kOutput, calls=%fused_computation.38 | convolution fusion | flops 6450839552 | bytes 16789504 | tf_op jit(solution)/shard_map/dot_general | solution.py:393
  419.0 1.9 slice_bitcast_fusion.3
  420.9 1.4 copy-done.4
  422.5 3.3 subtract_convert_fusion.1
  426.0 0.6 copy-done.14
  426.8 1.6 copy.99
  428.3 4.6 all-to-all-start.1
  433.0 0.7 all-gather.4.cloned.1.call-update
  433.7 10.6 %fusion.169 = (f32[4,1024]{1,0:T(4,128)S(1)}, f32[4,1024,1024]{1,2,0:T(8,128)}) fusion(pred[1024,1024]{0,1:T(8,128)(4,1)S(1)} %copy-done.19, bf16[1024,4,64]{0,2,1:T(8,128)(2,1)S(1)} %copy-done.15, bf16[1024,4,64]{0,2,1:T(8,128)(2,1)S(1)} %copy-done.17, bf16[1024,4,64]{0,2,1:T(8,128)(2,1)S(1)} %copy-done.25, bf16[1024,4,64]{0,2,1:T(8,128)(2,1)S(1)} %copy-done.24), kind=kOutput, calls=%fused_computation.265 | convolution fusion | flops 1094714368 | bytes 19939328 | tf_op jit(solution)/shard_map/sub | solution.py:354
  444.3 7.7 fusion.66
  452.1 1.3 copy.138.refs_0_
  453.6 3.9 fusion.24
  457.9 0.6 fusion.56
  458.9 0.4 fusion.54
  459.3 1.1 convolution_bitcast_fusion.refs_1_
  460.4 123.0 %ctx_gather.3 = (bf16[4,1024,512]{2,1,0:T(8,128)(2,1)}, bf16[8,2048]{1,0:T(8,128)(2,1)}) custom-call(bf16[1024,512]{1,0:T(8,128)(2,1)} %copy.138.refs_0_, f32[8,2048]{1,0:T(8,128)} %convolution_bitcast_fusion.refs_1_), custom_call_target="tpu_custom_call" | custom-call | flops 70000001024 | bytes 5242880 | tf_op jit(solution)/shard_map/ctx_gather/pallas_call | solution.py:108
  583.4 0.9 fusion.86
  584.4 7.3 fusion.48
  591.7 0.5 collective-permute-start.1
  592.2 4.3 fusion.30.refs_6_
  596.5 7.3 bitcast_select_fusion.1
  603.9 7.8 maximum_bitcast_fusion
  611.6 22.0 %collective-permute-done.1 = bf16[2,1024,4,128]{1,3,0,2:T(8,128)(2,1)S(1)} collective-permute-done((bf16[2,1024,4,128]{1,3,0,2:T(8,128)(2,1)}, bf16[2,1024,4,128]{1,3,0,2:T(8,128)(2,1)S(1)}, u32[]{:S(2)}, u32[]{:S(2)}) %collective-permute-start.1) | collective-permute-done | bytes 2097184 | tf_op jit(solution)/shard_map/ppermute | solution.py:411
  633.7 2.7 fusion.53
  636.4 4.2 copy.104
  640.6 2.5 copy.105
  643.1 176.8 %mlp_sum.3 = (bf16[1024,2048]{1,0:T(8,128)(2,1)}, bf16[8,2048]{1,0:T(8,128)(2,1)}) custom-call(bf16[4,1024,512]{2,1,0:T(8,128)(2,1)} %get-tuple-element.21.refs_0_, bf16[1024,2048]{1,0:T(8,128)(2,1)} %get-tuple-element.18.refs_1_, bf16[2048,2048]{1,0:T(8,128)(2,1)} %all-gather.4.cloned.1.call-done.refs_2_, bf16[2,2,1376,2048]{3,2,1,0:T(8,128)(2,1)} %refs_3_.3, ...), custom_call_target="tpu_custom_call" | custom-call | flops 160000000000 | bytes 41943040 | tf_op jit(solution)/shard_map/mlp_sum/pallas_call | solution.py:292
  820.0 1.4 fusion.89
  821.4 4.8 copy.186
  (132 shorter events, 3.8 us)
Async XLA Ops:
  7.2 219.6 %all-gather.6.cloned.1.call-start = ((), (), s32[]{:S(2)}) async-start(), calls=%async_computation.3 | async-start | bytes 8650752 | tf_op jit(solution)/shard_map/all_gather | solution.py:439
  33.2 3.4 copy-start.6
  45.7 2.7 copy-start.5
  49.6 0.7 copy-start.10
  49.6 1.0 copy-start.12
  52.1 173.1 %all-to-all-start = ((bf16[2,1024,4,128]{1,3,0,2:T(8,128)(2,1)}), bf16[2,1024,4,128]{1,3,0,2:T(8,128)(2,1)}, u32[]{:S(2)}, u32[]{:S(2)}) async-start(bf16[2,1024,4,128]{1,3,0,2:T(8,128)(2,1)} %copy.98), calls=%async_computation | async-start | bytes 4194304 | tf_op jit(solution)/shard_map/all_to_all | solution.py:410
  59.7 10.2 %copy-start.18 = (pred[1024,1024]{0,1:T(8,128)(4,1)}, pred[1024,1024]{0,1:T(8,128)(4,1)S(1)}, u32[]{:S(2)}) copy-start(pred[1024,1024]{0,1:T(8,128)(4,1)S(1)} %fusion.44) | copy-start | bytes 3145732
  59.7 10.2 %copy-start.43 = (s32[8]{0:T(128)S(1)}, s32[8]{0:T(128)}, u32[]{:S(2)}) copy-start(s32[8]{0:T(128)} %param.26) | copy-start | bytes 100
  69.9 9.1 %copy-start.20 = (bf16[8,2048]{1,0:T(8,128)(2,1)S(1)}, bf16[8,2048]{1,0:T(8,128)(2,1)}, u32[]{:S(2)}) copy-start(bf16[8,2048]{1,0:T(8,128)(2,1)} %param.23) | copy-start | bytes 98308
  69.9 9.3 %copy-start.38 = (f32[2,2,2048]{2,1,0:T(2,128)S(1)}, f32[2,2,2048]{2,1,0:T(2,128)}, u32[]{:S(2)}) copy-start(f32[2,2,2048]{2,1,0:T(2,128)} %param.31) | copy-start | bytes 98308
  79.2 11.7 %copy-start.31 = (f32[8,64]{1,0:T(8,128)}, f32[8,64]{1,0:T(8,128)S(1)}, u32[]{:S(2)}) copy-start(f32[8,64]{1,0:T(8,128)S(1)} %get-tuple-element.114) | copy-start | bytes 6148
  79.2 11.7 %copy-start.33 = (f32[8,64]{1,0:T(8,128)}, f32[8,64]{1,0:T(8,128)S(1)}, u32[]{:S(2)}) copy-start(f32[8,64]{1,0:T(8,128)S(1)} %get-tuple-element.115) | copy-start | bytes 6148
  90.0 2.2 copy-start.2
  91.9 3.6 copy-start.29
  92.2 3.5 copy-start
  95.6 2.9 copy-start.7
  204.3 10.7 %copy-start.26 = (bf16[8,2048]{1,0:T(8,128)(2,1)S(1)}, bf16[8,2048]{1,0:T(8,128)(2,1)}, u32[]{:S(2)}) copy-start(bf16[8,2048]{1,0:T(8,128)(2,1)} %get-tuple-element.17) | copy-start | bytes 98308
  225.2 386.4 %collective-permute-start = (bf16[2,1024,4,128]{1,3,0,2:T(8,128)(2,1)}, bf16[2,1024,4,128]{1,3,0,2:T(8,128)(2,1)}, u32[]{:S(2)}, u32[]{:S(2)}) collective-permute-start(bf16[2,1024,4,128]{1,3,0,2:T(8,128)(2,1)} %all-to-all-done), channel_id=1, source_target_pairs={{0,2},{1,3},{2,0},{3,1},{4,6},{5,7},{6,4},{7,5},{8,10},{9,11},{10,... | collective-permute-start | bytes 6291464 | tf_op jit(solution)/shard_map/ppermute | solution.py:411
  406.5 3.5 copy-start.9
  406.5 3.4 copy-start.42
  419.0 3.3 copy-start.4
  419.0 3.5 copy-start.11
  425.7 0.8 copy-start.14
  425.7 1.0 copy-start.16
  426.8 6.9 copy-start.19
  426.8 6.9 copy-start.24
  426.8 6.9 copy-start.25
  428.3 5.4 copy-start.15
  428.3 5.4 copy-start.17
  428.3 163.3 %all-to-all-start.1 = ((bf16[2,1024,4,128]{1,3,0,2:T(8,128)(2,1)}), bf16[2,1024,4,128]{1,3,0,2:T(8,128)(2,1)}, u32[]{:S(2)}, u32[]{:S(2)}) async-start(bf16[2,1024,4,128]{1,3,0,2:T(8,128)(2,1)} %copy.99), calls=%async_computation.1 | async-start | bytes 4194304 | tf_op jit(solution)/shard_map/all_to_all | solution.py:410
  432.9 210.2 %all-gather.4.cloned.1.call-start = ((), (), s32[]{:S(2)}) async-start(), calls=%async_computation.2 | async-start | bytes 8650752 | tf_op jit(solution)/shard_map/all_gather | solution.py:439
  444.3 9.1 %copy-start.21 = (bf16[8,2048]{1,0:T(8,128)(2,1)S(1)}, bf16[8,2048]{1,0:T(8,128)(2,1)}, u32[]{:S(2)}) copy-start(bf16[8,2048]{1,0:T(8,128)(2,1)} %param.23) | copy-start | bytes 98308
  444.3 9.1 %copy-start.27 = (bf16[8,2048]{1,0:T(8,128)(2,1)S(1)}, bf16[8,2048]{1,0:T(8,128)(2,1)}, u32[]{:S(2)}) copy-start(bf16[8,2048]{1,0:T(8,128)(2,1)} %get-tuple-element.17) | copy-start | bytes 98308
  444.3 9.1 %copy-start.39 = (bf16[8,2048]{1,0:T(8,128)(2,1)S(1)}, bf16[8,2048]{1,0:T(8,128)(2,1)}, u32[]{:S(2)}) copy-start(bf16[8,2048]{1,0:T(8,128)(2,1)} %get-tuple-element.20) | copy-start | bytes 98308
  444.3 9.3 %copy-start.37 = (f32[1,1,2048]{2,1,0:T(1,128)S(1)}, f32[1,1,2048]{2,1,0:T(1,128)}, u32[]{:S(2)}) copy-start(f32[1,1,2048]{2,1,0:T(1,128)} %get-tuple-element.89) | copy-start | bytes 24580
  452.0 5.5 copy-start.32
  452.1 5.5 copy-start.34
  452.1 5.8 copy-start.3
  453.6 130.8 %copy-start.22 = (bf16[8,2048]{1,0:T(8,128)(2,1)}, bf16[8,2048]{1,0:T(8,128)(2,1)S(1)}, u32[]{:S(2)}) copy-start(bf16[8,2048]{1,0:T(8,128)(2,1)S(1)} %get-tuple-element.47) | copy-start | bytes 98308
  453.6 4.9 copy-start.30
  453.6 5.3 copy-start.13
  453.6 5.7 copy-start.8
  460.4 124.0 %copy-start.40 = (f32[1,1,2048]{2,1,0:T(1,128)S(1)}, f32[1,1,2048]{2,1,0:T(1,128)}, u32[]{:S(2)}) copy-start(f32[1,1,2048]{2,1,0:T(1,128)} %get-tuple-element.86) | copy-start | bytes 24580
  591.6 4.9 copy-start.35
  591.6 4.9 copy-start.36
  591.6 4.9 copy-start.41
  591.7 4.8 copy-start.1
  591.7 42.0 %collective-permute-start.1 = (bf16[2,1024,4,128]{1,3,0,2:T(8,128)(2,1)}, bf16[2,1024,4,128]{1,3,0,2:T(8,128)(2,1)S(1)}, u32[]{:S(2)}, u32[]{:S(2)}) collective-permute-start(bf16[2,1024,4,128]{1,3,0,2:T(8,128)(2,1)} %all-to-all-done.1), channel_id=1, source_target_pairs={{0,2},{1,3},{2,0},{3,1},{4,6},{5,7},{6,4},{7,5},{8,10},{9,11},{10,... | collective-permute-start | bytes 6291464 | tf_op jit(solution)/shard_map/ppermute | solution.py:411
  643.1 176.8 %copy-start.23 = (bf16[8,2048]{1,0:T(8,128)(2,1)S(1)}, bf16[8,2048]{1,0:T(8,128)(2,1)}, u32[]{:S(2)}) copy-start(bf16[8,2048]{1,0:T(8,128)(2,1)} %copy-done.22) | copy-start | bytes 98308
  643.1 176.9 %copy-start.28 = (bf16[8,2048]{1,0:T(8,128)(2,1)S(1)}, bf16[8,2048]{1,0:T(8,128)(2,1)}, u32[]{:S(2)}) copy-start(bf16[8,2048]{1,0:T(8,128)(2,1)} %get-tuple-element.23) | copy-start | bytes 98308
Sparse Core Ops, SparseCore 0:
  10.8 108.5 all-gather.5
  436.6 99.3 all-gather.3

commit v3 on v2

--- a/solution.py
+++ b/solution.py
@@ -9,9 +9,10 @@
 THETA = 10000.0
 MASKED = -1e30
 CTX_ROWS = 128
-SUM_ROWS = 32
+SUM_ROWS = 16
 DOT_ROWS = 128
 DOT_COLS = 512
+STAGES = 4
 FF_COLS = 256
 SUM_VMEM_BYTES = 63 * 1024 * 1024
 VMEM_BYTES = 56 * 1024 * 1024
@@ -129,10 +130,11 @@
     loads = [
         pltpu.make_async_copy(ctx_hbm, ctx_ref, in_sems.at[0]),
         pltpu.make_async_copy(hid_hbm, hid_ref, in_sems.at[1]),
-        pltpu.make_async_copy(wo_hbm, wo_ref, in_sems.at[2]),
-        pltpu.make_async_copy(gu_hbm.at[layer], gu_ref, in_sems.at[3]),
-        pltpu.make_async_copy(wd_hbm.at[layer], wd_ref, in_sems.at[4]),
+        pltpu.make_async_copy(gu_hbm.at[layer], gu_ref, in_sems.at[2]),
+        pltpu.make_async_copy(wd_hbm.at[layer], wd_ref, in_sems.at[3]),
     ]
+    weight_loads = [pltpu.make_async_copy(wo_hbm.at[:, src], wo_ref.at[src], in_sems.at[4 + src]) for src in range(tp_size)]
+    loads = loads[:2] + weight_loads + loads[2:]
     for load in loads:
         load.start()
     greet(me, tp_size)
@@ -153,23 +155,25 @@
 
     def tick(time, carry):
         step = time - per_dot
-        stage = lax.rem(time, per_dot)
+        pace = per_dot // STAGES
+        on_beat = lax.rem(time, pace) == 0
+        stage = lax.rem(time, per_dot) // pace
         block = time // per_dot
-        working = time < chunks
+        working = (time < chunks) & on_beat
         block_rows = [pl.ds(pl.multiple_of(base + block * DOT_ROWS, DOT_ROWS), DOT_ROWS) for base in (half, 0)]
 
         @pl.when(time == 0)
         def _():
-            for load in loads[:3]:
+            for load in loads[:-2]:
                 load.wait()
 
-        @pl.when(time == 1)
-        def _():
-            loads[3].wait()
-
-        @pl.when(time == 3)
-        def _():
-            loads[4].wait()
+        @pl.when(time == pace)
+        def _():
+            loads[-2].wait()
+
+        @pl.when(time == 3 * pace)
+        def _():
+            loads[-1].wait()
 
         @pl.when(working & (stage == 0))
         def _():
@@ -178,7 +182,7 @@
                 attn = None
                 for src in range(tp_size):
                     both = jnp.concatenate([ctx_ref[src, rows, :] for rows in block_rows], axis=0)
-                    term = jnp.dot(both, wo_ref[src * shard:(src + 1) * shard, cols], preferred_element_type=jnp.float32)
+                    term = jnp.dot(both, wo_ref[src, :, :, cols].reshape(shard, DOT_COLS), preferred_element_type=jnp.float32)
                     attn = term if attn is None else attn + term
                 attn = attn.astype(jnp.bfloat16).astype(jnp.float32)
                 for idx_rows, rows in enumerate(block_rows):
@@ -297,7 +301,7 @@
         scratch_shapes=[
             pltpu.VMEM(ctx_full.shape, bf16),
             pltpu.VMEM((rows, width), bf16),
-            pltpu.VMEM(wo_full.shape, bf16),
+            pltpu.VMEM((wo_full.shape[1], wo_full.shape[0]) + wo_full.shape[2:], bf16),
             pltpu.VMEM((2, ff_loc, width), bf16),
             pltpu.VMEM((ff_loc, width), bf16),
             pltpu.VMEM((2 * DOT_ROWS, width), bf16),
@@ -305,7 +309,7 @@
             pltpu.VMEM((rows, width), jnp.float32),
             pltpu.VMEM((rows, width), jnp.float32),
             pltpu.VMEM((tp_size,) + small_part.shape, jnp.float32),
-            pltpu.SemaphoreType.DMA((5,)),
+            pltpu.SemaphoreType.DMA((4 + tp_size,)),
         ] + [pltpu.SemaphoreType.DMA((chunks,))] * 8 + [pltpu.SemaphoreType.DMA((tp_size - 1,)), pltpu.SemaphoreType.DMA((tp_size,))],
         compiler_params=pltpu.CompilerParams(collective_id=1 + layer, has_side_effects=True, vmem_limit_bytes=SUM_VMEM_BYTES),
         cost_estimate=pl.CostEstimate(flops=160_000_000_000, bytes_accessed=rows * width * 20, transcendentals=0),
@@ -370,7 +374,7 @@
     return context.astype(jnp.bfloat16)
 
 
-def run_layers(prompt, s_valid, w_qkv_pre, wo_parts, w_gu_pre, w_down_pre, gains_pre, tokens, k_cache, v_cache, c_len, w_qkv_dec, w_out_dec, w_gu_dec, w_down_dec, gains_dec, partner_perm, tp_size):
+def run_layers(prompt, s_valid, w_qkv_pre, wo_full, w_gu_pre, w_down_pre, gains_pre, tokens, k_cache, v_cache, c_len, w_qkv_dec, w_out_dec, w_gu_dec, w_down_dec, gains_dec, partner_perm, tp_size):
     layers, row_count, cache_len, heads_loc, _, head_dim = k_cache.shape
     width = tokens.shape[1]
     seq_len = prompt.shape[0]
@@ -403,40 +407,35 @@
         v_tok = qkv_tok[:, 2].astype(jnp.bfloat16)
         ctx_tok = decode_attention(q_tok, k_tok, v_tok, k_local[layer_idx], v_local[layer_idx], visible)
         part_tok = jnp.einsum('bhe,hed->bd', ctx_tok, wout_local[layer_idx], preferred_element_type=jnp.float32)
-        k_next.append(jnp.where(write_at, k_tok[:, None], k_local[layer_idx]))
-        v_next.append(jnp.where(write_at, v_tok[:, None], v_local[layer_idx]))
+        k_next.append(k_tok)
+        v_next.append(v_tok)
 
         ctx_full, attn_tok = gather_ctx(context, part_tok, tp_size)
-        kv_new = lax.all_to_all(jnp.stack([keys_new, values_new]), 'tp', 2, 2, tiled=True)
+        kv_new = jnp.stack([keys_new, values_new])
+        if layer_idx > 0:
+            kv_new, attn_tok = lax.optimization_barrier((kv_new, attn_tok))
+        kv_new = lax.all_to_all(kv_new, 'tp', 2, 2, tiled=True)
         installed.append(lax.ppermute(kv_new, 'side', partner_perm))
-
-        if layer_idx == 0:
-            wo_full = gather_wo(wo_parts[0])
-        else:
-            wo_full = gather_wo(wo_next)
         tokens = add_residual(tokens, attn_tok)
         act_tok = swiglu(tokens, gains_dec[layer_idx, 1], w_gu_dec[layer_idx])
         mlp_tok = jnp.einsum('bf,fd->bd', act_tok, w_down_dec[layer_idx], preferred_element_type=jnp.float32)
-        hidden, down_tok = mlp_and_sum(layer_idx, ctx_full, hidden, wo_full, w_gu_pre, w_down_pre, gains_pre[layer_idx, 1][None], mlp_tok, tp_size)
-        if layer_idx + 1 < layers:
-            wo_next, down_tok = lax.optimization_barrier((wo_parts[layer_idx + 1], down_tok))
+        hidden, down_tok = mlp_and_sum(layer_idx, ctx_full, hidden, wo_full[layer_idx], w_gu_pre, w_down_pre, gains_pre[layer_idx, 1][None], mlp_tok, tp_size)
         tokens = add_residual(tokens, down_tok)
-    k_new = jnp.stack(k_next).reshape(k_cache.shape)
-    v_new = jnp.stack(v_next).reshape(v_cache.shape)
+    hidden, installed[-1] = lax.optimization_barrier((hidden, installed[-1]))
+    write_rows = write_at[None]
+    k_new = jnp.where(write_rows, jnp.stack(k_next)[:, :, None], k_local).reshape(k_cache.shape)
+    v_new = jnp.where(write_rows, jnp.stack(v_next)[:, :, None], v_local).reshape(v_cache.shape)
     return hidden, tokens, installed, k_new, v_new
 
 
-def parts_of_wo(w_out, side_size, pair_size):
+def gather_wo(w_out, side_size, pair_size):
     layers, heads_loc, head_dim, width = w_out.shape
     rows = heads_loc * head_dim
-    part = rows // (side_size * pair_size)
+    copies = side_size * pair_size
     place = lax.axis_index('pair') * side_size + lax.axis_index('side')
-    flat = w_out.reshape(layers, rows, width)
-    return [lax.dynamic_slice(flat, (layer_idx, place * part, 0), (1, part, width))[0] for layer_idx in range(layers)]
-
-
-def gather_wo(part):
-    return lax.all_gather(part, ('tp', 'pair', 'side'), axis=0, tiled=True)
+    mine = lax.dynamic_index_in_dim(w_out.reshape(layers, copies, rows // copies, width), place, axis=1, keepdims=False)
+    line = lax.all_gather(mine.reshape(-1, width), 'tp', axis=0).reshape(-1, layers, rows // copies, width)
+    return [lax.all_gather(line[:, layer_idx], ('pair', 'side'), axis=0) for layer_idx in range(layers)]
 
 
 def solution(mesh):
@@ -453,8 +452,8 @@
     out_specs = (rows_spec, rows_spec, prompt_spec, prompt_spec, cache_spec, cache_spec)
 
     def device_fn(prompt_x, s_len, w_qkv_pre, w_out_pre, w_gu_pre, w_down_pre, gain_pre, dec_tokens, k_cache, v_cache, c_len, w_qkv_dec, w_out_dec, w_gu_dec, w_down_dec, gain_dec):
-        wo_parts = parts_of_wo(w_out_pre, side_size, pair_size)
-        hidden, dec_out, installed, k_cache_new, v_cache_new = run_layers(prompt_x, s_len, w_qkv_pre, wo_parts, w_gu_pre, w_down_pre, gain_pre, dec_tokens, k_cache, v_cache, c_len, w_qkv_dec, w_out_dec, w_gu_dec, w_down_dec, gain_dec, partner_perm, tp_size)
+        wo_full = gather_wo(w_out_pre, side_size, pair_size)
+        hidden, dec_out, installed, k_cache_new, v_cache_new = run_layers(prompt_x, s_len, w_qkv_pre, wo_full, w_gu_pre, w_down_pre, gain_pre, dec_tokens, k_cache, v_cache, c_len, w_qkv_dec, w_out_dec, w_gu_dec, w_down_dec, gain_dec, partner_perm, tp_size)
         prompt_kv = jnp.stack(installed, axis=1)[:, :, :, :, None, :]
         return hidden, dec_out, prompt_kv[0], prompt_kv[1], k_cache_new, v_cache_new
 

time: 841 us -> 785 us (0.933)
  Pallas kernels: 583 us -> 534 us
    pallas_call x2, Pallas kernels: 227 us -> 153 us  [gather_ctx(): pl.pallas_call(lambda *refs: ctx_kernel(tp_size, *refs), out_shape=(jax.S...]
    pallas_call x2, Pallas kernels: 357 us -> 381 us  [mlp_and_sum(): pl.pallas_call(lambda *refs: sum_kernel(layer, tp_size, *refs), out_shape...]
    ppermute x2, waiting for transfers between devices: 22.1 us -> 0.01 us  [run_layers(): installed.append(lax.ppermute(kv_new, 'side', partner_perm))]
    all_to_all x2, waiting for transfers between devices: 0.01 us -> 17.1 us  [run_layers(): kv_new = lax.all_to_all(kv_new, 'tp', 2, 2, tiled=True)]
    unnamed x91 -> x95, local copies, waits for them, and re-layouts: 17.1 us -> 16.5 us
  transfers between devices with their start and end apart: 6 -> 7, of which waited for: 1 -> 1; matrix products, arithmetic and copies ran while one was open for 22% -> 22% of each run, Pallas kernels for 49% -> 69%
where the time goes in v3:
time: 785 us; the launch traced here: 773 us
  Pallas kernels  534 us (68%)
  matrix products  85 us (11%)
  local copies, waits for them, and re-layouts  82.2 us (10%)
  other arithmetic  26.5 us (3%)
  waiting for transfers between devices  17.2 us (2%)
  between operations  15.5 us (2%)
  starting transfers between devices  12.9 us (2%)
    pallas_call x2, Pallas kernels, mlp_and_sum(): pl.pallas_call(lambda *refs: sum_kernel(layer, tp_size, *refs), out_shape...  381 us
    pallas_call x2, Pallas kernels, gather_ctx(): pl.pallas_call(lambda *refs: ctx_kernel(tp_size, *refs), out_shape=(jax.S...  153 us
    squeeze x2, local copies, waits for them, and re-layouts, run_layers(): wqkv_flat[layer_idx]  21.3 us
    sub x2, matrix products, prompt_attention(): prob_bf = jax.nn.softmax(scores, axis=-1).astype(jnp.bfloat16)  20.2 us
    dot_general x2, matrix products, run_layers(): jnp.dot(normed, wqkv_flat[layer_idx], preferred_element_type=jnp.float32)  18.1 us
    all_to_all x2, waiting for transfers between devices, run_layers(): kv_new = lax.all_to_all(kv_new, 'tp', 2, 2, tiled=True)  17.1 us
    unnamed x95, local copies, waits for them, and re-layouts  16.5 us
    dot_general x2, matrix products, prompt_attention(): jnp.einsum('hqk,khe->qhe', prob_bf, values_in, preferred_element_type=jnp...  16.4 us
  transfers between devices with their start and end apart: 7, of which 1 were waited for; matrix products, arithmetic and copies ran while one was open for 22% of the time, Pallas kernels for 69%

profile of v3, /device:TPU:0, one launch (start us, length us, event | category | flops | bytes accessed | tf_op | source)
XLA Modules:
  0.0 773.4 jit_solution(901511303924799134)
XLA Ops:
  7.2 1.9 constant_dynamic-slice_fusion
  9.1 1.4 slice_bitcast_fusion.16
  10.6 12.0 %fusion.170 = (bf16[1,2048,3,4,128]{4,3,2,1,0:T(4,128)(2,1)}, bf16[1,2048,3,4,128]{4,3,2,1,0:T(4,128)(2,1)}) fusion(bf16[2,2048,3,4,128]{4,3,2,1,0:T(4,128)(2,1)} %param.18), kind=kLoop, calls=%fused_computation.261 | loop fusion | bytes 25165824 | tf_op jit(solution)/shard_map/slice | solution.py:397
  22.6 10.6 %copy.141 = bf16[1,2048,3,4,128]{1,4,3,2,0:T(8,128)(2,1)} copy(bf16[1,2048,3,4,128]{4,3,2,1,0:T(4,128)(2,1)} %get-tuple-element.58) | data formatting | bytes 12582912 | tf_op jit(solution)/shard_map/squeeze | solution.py:397
  33.2 3.2 fusion.10
  36.6 9.0 %fusion.28 = f32[1024,3,4,128]{0,3,2,1:T(8,128)S(1)} fusion(bf16[1,2048,3,4,128]{1,4,3,2,0:T(8,128)(2,1)} %copy.141, bf16[1024,2048]{1,0:T(8,128)(2,1)S(1)} %copy-done.5, f32[2048]{0:T(1024)S(1)} %bitcast.227, f32[1024]{0:T(1024)S(1)} %add_rsqrt_fusion.1), kind=kOutput, calls=%fused_computation.40 | convolution fusion | flops 6450839552 | bytes 16789504 | tf_op jit(solution)/shard_map/dot_general | solution.py:397
  45.7 1.0 multiply_cosine_fusion
  46.9 0.3 slice_bitcast_fusion.7
  47.2 1.1 copy-done.4
  48.5 0.7 subtract_convert_fusion.3
  49.4 1.6 copy.108
  50.9 6.4 all-to-all-start.1
  58.0 0.4 fusion.44
  58.3 10.1 %fusion.173 = (f32[4,1024]{1,0:T(4,128)S(1)}, f32[4,1024,1024]{1,2,0:T(8,128)}) fusion(pred[1024,1024]{0,1:T(8,128)(4,1)S(1)} %fusion.44, bf16[1024,4,64]{0,2,1:T(8,128)(2,1)S(1)} %get-tuple-element.82, bf16[1024,4,64]{0,2,1:T(8,128)(2,1)S(1)} %get-tuple-element.83, bf16[1024,4,64]{0,2,1:T(8,128)(2,1)S(1)} %get-tuple-element.75, ...), kind=kOutput, calls=%fused_computation.264 | convolution fusion | flops 1094714368 | bytes 19939328 | tf_op jit(solution)/shard_map/sub | solution.py:358
  68.5 3.1 fusion.171
  71.6 0.2 all-gather.10.cloned.1.call-start
  71.8 7.7 fusion.67
  79.5 1.3 copy.142.refs_0_
  80.9 10.6 %copy.144 = bf16[1,2048,3,4,128]{1,4,3,2,0:T(8,128)(2,1)} copy(bf16[1,2048,3,4,128]{4,3,2,1,0:T(4,128)(2,1)} %get-tuple-element.59) | data formatting | bytes 12582912 | tf_op jit(solution)/shard_map/squeeze | solution.py:397
  91.8 0.6 fusion.172
  92.4 10.1 %fusion.169 = (bf16[1,2048,3,4,1,128]{5,3,4,2,1,0:T(4,128)(2,1)}, bf16[1,2048,3,4,1,128]{5,3,4,2,1,0:T(4,128)(2,1)S(1)}) fusion(bf16[2,2048,3,4,1,128]{5,3,4,2,1,0:T(4,128)(2,1)} %param.27), kind=kLoop, calls=%fused_computation.260 | loop fusion | bytes 25165824 | tf_op jit(solution)/shard_map/slice | solution.py:404
  102.5 1.0 fusion.25
  103.9 0.7 iota_compare_fusion.1
  104.7 2.4 slice_bitcast_fusion.9
  107.2 0.6 fusion.60
  108.2 2.5 slice_bitcast_fusion.8
  110.7 0.4 fusion.58
  111.1 1.0 convolution_bitcast_fusion.1.refs_1_
  112.2 80.4 %ctx_gather.2 = (bf16[4,1024,512]{2,1,0:T(8,128)(2,1)}, bf16[8,2048]{1,0:T(8,128)(2,1)}) custom-call(bf16[1024,512]{1,0:T(8,128)(2,1)} %copy.142.refs_0_, f32[8,2048]{1,0:T(8,128)} %convolution_bitcast_fusion.1.refs_1_), custom_call_target="tpu_custom_call" | custom-call | flops 70000001024 | bytes 5242880 | tf_op jit(solution)/shard_map/ctx_gather/pallas_call | solution.py:109
  192.6 0.9 fusion.78
  193.5 7.3 fusion.45
  200.8 4.1 fusion.32.refs_6_
  204.9 193.5 %mlp_sum.2 = (bf16[1024,2048]{1,0:T(8,128)(2,1)}, bf16[8,2048]{1,0:T(8,128)(2,1)}) custom-call(bf16[4,1024,512]{2,1,0:T(8,128)(2,1)} %get-tuple-element.18.refs_0_, bf16[1024,2048]{1,0:T(8,128)(2,1)} %refs_1_.1, bf16[8,4,64,2048]{3,2,1,0:T(8,128)(2,1)} %bitcast.229, bf16[2,2,1376,2048]{3,2,1,0:T(8,128)(2,1)} %refs_3_.3, bf16[2,1376,2048]{2,1,0:T(8,128)(2,1)} %refs_4_.3, ...), custom_call_target="tpu_custom_call" | custom-call | flops 160000000000 | bytes 41943040 | tf_op jit(solution)/shard_map/mlp_sum/pallas_call | solution.py:296
  398.4 3.2 fusion.13
  401.9 9.0 %fusion.26 = f32[1024,3,4,128]{0,3,2,1:T(8,128)S(1)} fusion(bf16[1,2048,3,4,128]{1,4,3,2,0:T(8,128)(2,1)} %copy.144, bf16[1024,2048]{1,0:T(8,128)(2,1)S(1)} %copy-done.8, f32[2048]{0:T(1024)S(1)} %bitcast.226, f32[1024]{0:T(1024)S(1)} %add_rsqrt_fusion), kind=kOutput, calls=%fused_computation.38 | convolution fusion | flops 6450839552 | bytes 16789504 | tf_op jit(solution)/shard_map/dot_general | solution.py:397
  411.0 0.3 slice_bitcast_fusion.3
  411.3 2.3 copy-done.3
  413.6 0.7 subtract_convert_fusion.1
  414.4 0.5 copy-done.15
  414.8 10.1 %fusion.174 = (f32[4,1024]{1,0:T(4,128)S(1)}, f32[4,1024,1024]{1,2,0:T(8,128)}) fusion(pred[1024,1024]{0,1:T(8,128)(4,1)S(1)} %copy-done.15, bf16[1024,4,64]{0,2,1:T(8,128)(2,1)S(1)} %get-tuple-element.80, bf16[1024,4,64]{0,2,1:T(8,128)(2,1)S(1)} %get-tuple-element.81, bf16[1024,4,64]{0,2,1:T(8,128)(2,1)S(1)} %get-tuple-element.71, ...), kind=kOutput, calls=%fused_computation.265 | convolution fusion | flops 1094714368 | bytes 19939328 | tf_op jit(solution)/shard_map/sub | solution.py:358
  425.0 8.7 %fusion.66 = bf16[4,128,1024]{2,1,0:T(8,128)(2,1)} fusion(f32[4,1024,1024]{1,2,0:T(8,128)} %get-tuple-element.123, f32[4,1024]{1,0:T(4,128)S(1)} %get-tuple-element.122, f32[1024,3,4,128]{0,3,2,1:T(8,128)} %copy-done.3), kind=kOutput, calls=%fused_computation.92 | convolution fusion | flops 1082654720 | bytes 18890752 | tf_op jit(solution)/shard_map/hqk,khe->qhe/dot_general | solution.py:359
  433.7 2.7 copy.145.refs_0_
  436.6 3.9 fusion.24
  440.8 0.6 fusion.56
  441.9 0.4 fusion.54
  442.3 1.1 convolution_bitcast_fusion.refs_1_
  443.4 73.0 %ctx_gather.3 = (bf16[4,1024,512]{2,1,0:T(8,128)(2,1)}, bf16[8,2048]{1,0:T(8,128)(2,1)}) custom-call(bf16[1024,512]{1,0:T(8,128)(2,1)} %copy.145.refs_0_, f32[8,2048]{1,0:T(8,128)} %convolution_bitcast_fusion.refs_1_), custom_call_target="tpu_custom_call" | custom-call | flops 70000001024 | bytes 5242880 | tf_op jit(solution)/shard_map/ctx_gather/pallas_call | solution.py:109
  516.3 1.7 fusion.73
  518.1 0.2 pad_maximum_fusion.1
  518.3 1.6 copy.107
  519.9 4.4 all-to-all-start
  524.3 0.9 collective-permute-start.1
  525.4 5.8 fusion.48
  531.3 4.1 fusion.30.refs_6_
  535.4 17.1 %all-to-all-done = bf16[2,1024,4,128]{1,3,0,2:T(8,128)(2,1)} async-done(((bf16[2,1024,4,128]{1,3,0,2:T(8,128)(2,1)}), bf16[2,1024,4,128]{1,3,0,2:T(8,128)(2,1)}, u32[]{:S(2)}, u32[]{:S(2)}) %all-to-all-start) | async-done | bytes 2097184 | tf_op jit(solution)/shard_map/all_to_all | solution.py:417
  552.5 0.9 collective-permute-start
  553.5 187.2 %mlp_sum.3 = (bf16[1024,2048]{1,0:T(8,128)(2,1)}, bf16[8,2048]{1,0:T(8,128)(2,1)}) custom-call(bf16[4,1024,512]{2,1,0:T(8,128)(2,1)} %get-tuple-element.22.refs_0_, bf16[1024,2048]{1,0:T(8,128)(2,1)} %get-tuple-element.20.refs_1_, bf16[8,4,64,2048]{3,2,1,0:T(8,128)(2,1)} %bitcast.228, bf16[2,2,1376,2048]{3,2,1,0:T(8,128)(2,1)} %refs_3_.3, ...), custom_call_target="tpu_custom_call" | custom-call | flops 160000000000 | bytes 41943040 | tf_op jit(solution)/shard_map/mlp_sum/pallas_call | solution.py:296
  740.8 0.7 fusion.144
  741.6 1.4 fusion.89
  743.0 8.5 %broadcast_select_fusion = (bf16[2,8,256,4,1,128]{5,3,4,2,1,0:T(4,128)(2,1)}, bf16[2,8,256,4,1,128]{5,3,4,2,1,0:T(4,128)(2,1)}) fusion(bf16[2,8,256,4,1,128]{5,3,4,2,1,0:T(4,128)(2,1)} %param.25, pred[8,256]{1,0:T(8,128)(4,1)S(1)} %copy-done.43, bf16[2,8,4,128]{3,2,1,0:T(4,128)(2,1)S(1)} %copy.110, bf16[2,8,256,4,1,128]{5,3,4,2,1,0:T(4,128)(2,1)} %param.24, ...), kind=kLoop, calls=%fused_computation.58 | loop fusion | flops 4194304 | bytes 16812032 | tf_op jit(solution)/shard_map/jit(_where)/select_n | solution.py:427
  751.5 3.3 fusion.53
  754.8 4.2 copy.111
  759.1 2.5 copy.112
  761.6 4.8 copy.194
  (138 shorter events, 3.6 us)
Async XLA Ops:
  7.2 61.3 %all-gather.6.cloned.1.call-start = ((), (), s32[]{:S(2)}) async-start(), calls=%async_computation.2 | async-start | bytes 2621440 | tf_op jit(solution)/shard_map/all_gather | solution.py:437
  33.2 3.4 copy-start.5
  45.7 2.6 copy-start.4
  46.7 1.6 copy-start.9
  46.7 1.7 copy-start.11
  49.4 8.0 %copy-start.45 = (s32[8]{0:T(128)S(1)}, s32[8]{0:T(128)}, u32[]{:S(2)}) copy-start(s32[8]{0:T(128)} %param.26) | copy-start | bytes 100
  50.9 469.0 %all-to-all-start.1 = ((bf16[2,1024,4,128]{1,3,0,2:T(8,128)(2,1)}), bf16[2,1024,4,128]{1,3,0,2:T(8,128)(2,1)}, u32[]{:S(2)}, u32[]{:S(2)}) async-start(bf16[2,1024,4,128]{1,3,0,2:T(8,128)(2,1)} %copy.108), calls=%async_computation.1 | async-start | bytes 4194304 | tf_op jit(solution)/shard_map/all_to_all | solution.py:417
  57.3 147.6 %all-gather.8.cloned.1.call-start = ((), (), s32[]{:S(2)}) async-start(), calls=%async_computation.3 | async-start | bytes 9437184 | tf_op jit(solution)/shard_map/all_gather | solution.py:438
  58.3 10.1 %copy-start.14 = (pred[1024,1024]{0,1:T(8,128)(4,1)}, pred[1024,1024]{0,1:T(8,128)(4,1)S(1)}, u32[]{:S(2)}) copy-start(pred[1024,1024]{0,1:T(8,128)(4,1)S(1)} %fusion.44) | copy-start | bytes 3145732
  71.6 481.9 %all-gather.10.cloned.1.call-start = ((), (), s32[]{:S(2)}) async-start(), calls=%async_computation.4 | async-start | bytes 9437184 | tf_op jit(solution)/shard_map/all_gather | solution.py:438
  80.9 10.6 %copy-start.16 = (bf16[8,2048]{1,0:T(8,128)(2,1)S(1)}, bf16[8,2048]{1,0:T(8,128)(2,1)}, u32[]{:S(2)}) copy-start(bf16[8,2048]{1,0:T(8,128)(2,1)} %param.23) | copy-start | bytes 98308
  80.9 10.9 %copy-start.40 = (f32[2,2,2048]{2,1,0:T(2,128)S(1)}, f32[2,2,2048]{2,1,0:T(2,128)}, u32[]{:S(2)}) copy-start(f32[2,2,2048]{2,1,0:T(2,128)} %param.31) | copy-start | bytes 98308
  91.8 11.7 %copy-start.35 = (f32[8,64]{1,0:T(8,128)}, f32[8,64]{1,0:T(8,128)S(1)}, u32[]{:S(2)}) copy-start(f32[8,64]{1,0:T(8,128)S(1)} %get-tuple-element.116) | copy-start | bytes 6148
  91.8 11.7 %copy-start.37 = (f32[8,64]{1,0:T(8,128)}, f32[8,64]{1,0:T(8,128)S(1)}, u32[]{:S(2)}) copy-start(f32[8,64]{1,0:T(8,128)S(1)} %get-tuple-element.117) | copy-start | bytes 6148
  102.5 2.2 copy-start.1
  103.5 7.6 copy-start.23
  103.6 3.6 copy-start.27
  103.6 3.6 copy-start.29
  104.7 3.4 copy-start.25
  104.7 3.5 copy-start
  108.2 2.9 copy-start.6
  398.4 3.5 copy-start.8
  398.4 3.4 copy-start.44
  410.9 2.7 copy-start.3
  410.9 2.7 copy-start.10
  410.9 2.7 copy-start.12
  413.6 1.2 copy-start.15
  425.0 11.4 %copy-start.17 = (bf16[8,2048]{1,0:T(8,128)(2,1)S(1)}, bf16[8,2048]{1,0:T(8,128)(2,1)}, u32[]{:S(2)}) copy-start(bf16[8,2048]{1,0:T(8,128)(2,1)} %param.23) | copy-start | bytes 98308
  425.0 11.4 %copy-start.22 = (bf16[8,2048]{1,0:T(8,128)(2,1)S(1)}, bf16[8,2048]{1,0:T(8,128)(2,1)}, u32[]{:S(2)}) copy-start(bf16[8,2048]{1,0:T(8,128)(2,1)} %get-tuple-element.19) | copy-start | bytes 98308
  425.0 11.4 %copy-start.41 = (bf16[8,2048]{1,0:T(8,128)(2,1)S(1)}, bf16[8,2048]{1,0:T(8,128)(2,1)}, u32[]{:S(2)}) copy-start(bf16[8,2048]{1,0:T(8,128)(2,1)} %get-tuple-element.21) | copy-start | bytes 98308
  425.0 11.6 %copy-start.39 = (f32[1,1,2048]{2,1,0:T(1,128)S(1)}, f32[1,1,2048]{2,1,0:T(1,128)}, u32[]{:S(2)}) copy-start(f32[1,1,2048]{2,1,0:T(1,128)} %get-tuple-element.91) | copy-start | bytes 24580
  433.7 6.8 copy-start.36
  433.7 6.8 copy-start.38
  433.7 7.2 copy-start.2
  436.5 88.9 %copy-start.18 = (bf16[8,2048]{1,0:T(8,128)(2,1)}, bf16[8,2048]{1,0:T(8,128)(2,1)S(1)}, u32[]{:S(2)}) copy-start(bf16[8,2048]{1,0:T(8,128)(2,1)S(1)} %get-tuple-element.55) | copy-start | bytes 98308
  436.5 4.9 copy-start.26
  436.5 5.3 copy-start.13
  436.6 5.7 copy-start.7
  440.5 1.8 copy-start.24
  440.6 1.7 copy-start.31
  440.6 1.7 copy-start.33
  518.3 7.0 copy-start.20
  518.3 7.1 copy-start.42
  519.9 32.6 %all-to-all-start = ((bf16[2,1024,4,128]{1,3,0,2:T(8,128)(2,1)}), bf16[2,1024,4,128]{1,3,0,2:T(8,128)(2,1)}, u32[]{:S(2)}, u32[]{:S(2)}) async-start(bf16[2,1024,4,128]{1,3,0,2:T(8,128)(2,1)} %copy.107), calls=%async_computation | async-start | bytes 4194304 | tf_op jit(solution)/shard_map/all_to_all | solution.py:417
  524.3 227.2 %collective-permute-start.1 = (bf16[2,1024,4,128]{1,3,0,2:T(8,128)(2,1)}, bf16[2,1024,4,128]{1,3,0,2:T(8,128)(2,1)}, u32[]{:S(2)}, u32[]{:S(2)}) collective-permute-start(bf16[2,1024,4,128]{1,3,0,2:T(8,128)(2,1)} %all-to-all-done.1), channel_id=1, source_target_pairs={{0,2},{1,3},{2,0},{3,1},{4,6},{5,7},{6,4},{7,5},{8,10},{9,11},{10,... | collective-permute-start | bytes 6291464 | tf_op jit(solution)/shard_map/ppermute | solution.py:418
  552.5 199.0 %collective-permute-start = (bf16[2,1024,4,128]{1,3,0,2:T(8,128)(2,1)}, bf16[2,1024,4,128]{1,3,0,2:T(8,128)(2,1)}, u32[]{:S(2)}, u32[]{:S(2)}) collective-permute-start(bf16[2,1024,4,128]{1,3,0,2:T(8,128)(2,1)} %all-to-all-done), channel_id=1, source_target_pairs={{0,2},{1,3},{2,0},{3,1},{4,6},{5,7},{6,4},{7,5},{8,10},{9,11},{10,... | collective-permute-start | bytes 6291464 | tf_op jit(solution)/shard_map/ppermute | solution.py:418
  553.5 187.2 %copy-start.28 = (bf16[8,4,64]{2,0,1:T(8,128)(2,1)S(1)}, bf16[8,4,64]{2,0,1:T(8,128)(2,1)}, u32[]{:S(2)}) copy-start(bf16[8,4,64]{2,0,1:T(8,128)(2,1)} %copy-done.27) | copy-start | bytes 12292
  553.5 187.2 %copy-start.30 = (bf16[8,4,64]{2,0,1:T(8,128)(2,1)S(1)}, bf16[8,4,64]{2,0,1:T(8,128)(2,1)}, u32[]{:S(2)}) copy-start(bf16[8,4,64]{2,0,1:T(8,128)(2,1)} %copy-done.29) | copy-start | bytes 12292
  553.5 187.2 %copy-start.32 = (bf16[8,4,64]{2,0,1:T(8,128)(2,1)S(1)}, bf16[8,4,64]{2,0,1:T(8,128)(2,1)}, u32[]{:S(2)}) copy-start(bf16[8,4,64]{2,0,1:T(8,128)(2,1)} %copy-done.31) | copy-start | bytes 12292
  553.5 187.2 %copy-start.34 = (bf16[8,4,64]{2,0,1:T(8,128)(2,1)S(1)}, bf16[8,4,64]{2,0,1:T(8,128)(2,1)}, u32[]{:S(2)}) copy-start(bf16[8,4,64]{2,0,1:T(8,128)(2,1)} %copy-done.33) | copy-start | bytes 12292
  553.5 188.1 %copy-start.19 = (bf16[8,2048]{1,0:T(8,128)(2,1)S(1)}, bf16[8,2048]{1,0:T(8,128)(2,1)}, u32[]{:S(2)}) copy-start(bf16[8,2048]{1,0:T(8,128)(2,1)} %copy-done.18) | copy-start | bytes 98308
  553.5 188.1 %copy-start.21 = (bf16[8,2048]{1,0:T(8,128)(2,1)S(1)}, bf16[8,2048]{1,0:T(8,128)(2,1)}, u32[]{:S(2)}) copy-start(bf16[8,2048]{1,0:T(8,128)(2,1)} %get-tuple-element.24) | copy-start | bytes 98308
  553.5 189.5 %copy-start.43 = (pred[8,256]{1,0:T(8,128)(4,1)S(1)}, pred[8,256]{1,0:T(8,128)(4,1)}, u32[]{:S(2)}) copy-start(pred[8,256]{1,0:T(8,128)(4,1)} %get-tuple-element.118) | copy-start | bytes 6148
Sparse Core Ops, SparseCore 0:
  10.1 48.0 all-gather.5
  71.7 55.3 all-gather.7
  205.0 52.9 all-gather.9

commit v4 on v3

--- a/solution.py
+++ b/solution.py
@@ -9,7 +9,7 @@
 THETA = 10000.0
 MASKED = -1e30
 CTX_ROWS = 128
-SUM_ROWS = 16
+SUM_ROWS = 32
 DOT_ROWS = 128
 DOT_COLS = 512
 STAGES = 4
@@ -412,10 +412,13 @@
 
         ctx_full, attn_tok = gather_ctx(context, part_tok, tp_size)
         kv_new = jnp.stack([keys_new, values_new])
-        if layer_idx > 0:
+        if layer_idx == 0:
+            kv_new = lax.all_to_all(kv_new, 'tp', 2, 2, tiled=True)
+            installed.append(lax.ppermute(kv_new, 'side', partner_perm))
+        else:
+            kv_new = lax.ppermute(kv_new, 'side', partner_perm)
             kv_new, attn_tok = lax.optimization_barrier((kv_new, attn_tok))
-        kv_new = lax.all_to_all(kv_new, 'tp', 2, 2, tiled=True)
-        installed.append(lax.ppermute(kv_new, 'side', partner_perm))
+            installed.append(lax.all_to_all(kv_new, 'tp', 2, 2, tiled=True))
         tokens = add_residual(tokens, attn_tok)
         act_tok = swiglu(tokens, gains_dec[layer_idx, 1], w_gu_dec[layer_idx])
         mlp_tok = jnp.einsum('bf,fd->bd', act_tok, w_down_dec[layer_idx], preferred_element_type=jnp.float32)

time: 785 us -> 747 us (0.952)
  waiting for transfers between devices: 17.2 us -> 0.06 us
  Pallas kernels: 534 us -> 519 us
    all_to_all x2 -> x1, waiting for transfers between devices: 17.1 us -> 0.01 us  [run_layers(): kv_new = lax.all_to_all(kv_new, 'tp', 2, 2, tiled=True)]
    pallas_call x2, Pallas kernels: 381 us -> 367 us  [mlp_and_sum(): pl.pallas_call(lambda *refs: sum_kernel(layer, tp_size, *refs), out_shape...]
    unnamed x95 -> x89, local copies, waits for them, and re-layouts: 16.5 us -> 16 us
  transfers between devices with their start and end apart: 7 -> 7, of which waited for: 1 -> 0; matrix products, arithmetic and copies ran while one was open for 22% -> 23% of each run, Pallas kernels for 69% -> 70%
where the time goes in v4:
time: 747 us; the launch traced here: 737 us
  Pallas kernels  519 us (69%)
  matrix products  82.9 us (11%)
  local copies, waits for them, and re-layouts  80.4 us (11%)
  other arithmetic  26 us (3%)
  between operations  15.5 us (2%)
  starting transfers between devices  13.2 us (2%)
    pallas_call x2, Pallas kernels, mlp_and_sum(): pl.pallas_call(lambda *refs: sum_kernel(layer, tp_size, *refs), out_shape...  367 us
    pallas_call x2, Pallas kernels, gather_ctx(): pl.pallas_call(lambda *refs: ctx_kernel(tp_size, *refs), out_shape=(jax.S...  152 us
    squeeze x2, local copies, waits for them, and re-layouts, run_layers(): wqkv_flat[layer_idx]  21.3 us
    sub x2, matrix products, prompt_attention(): prob_bf = jax.nn.softmax(scores, axis=-1).astype(jnp.bfloat16)  20.3 us
    dot_general x2, matrix products, run_layers(): jnp.dot(normed, wqkv_flat[layer_idx], preferred_element_type=jnp.float32)  18.3 us
    unnamed x89, local copies, waits for them, and re-layouts  16 us
    dot_general x2, matrix products, prompt_attention(): jnp.einsum('hqk,khe->qhe', prob_bf, values_in, preferred_element_type=jnp...  15.4 us
  transfers between devices with their start and end apart: 7, of which 0 were waited for; matrix products, arithmetic and copies ran while one was open for 23% of the time, Pallas kernels for 70%

profile of v4, /device:TPU:0, one launch (start us, length us, event | category | flops | bytes accessed | tf_op | source)
XLA Modules:
  0.0 737.1 jit_solution(16597165992657230514)
XLA Ops:
  7.2 1.9 constant_dynamic-slice_fusion
  9.1 1.4 slice_bitcast_fusion.16
  10.6 12.0 %fusion.170 = (bf16[1,2048,3,4,128]{4,3,2,1,0:T(4,128)(2,1)}, bf16[1,2048,3,4,128]{4,3,2,1,0:T(4,128)(2,1)}) fusion(bf16[2,2048,3,4,128]{4,3,2,1,0:T(4,128)(2,1)} %param.18), kind=kLoop, calls=%fused_computation.261 | loop fusion | bytes 25165824 | tf_op jit(solution)/shard_map/slice | solution.py:397
  22.6 10.7 %copy.141 = bf16[1,2048,3,4,128]{1,4,3,2,0:T(8,128)(2,1)} copy(bf16[1,2048,3,4,128]{4,3,2,1,0:T(4,128)(2,1)} %get-tuple-element.58) | data formatting | bytes 12582912 | tf_op jit(solution)/shard_map/squeeze | solution.py:397
  33.2 3.2 fusion.10
  36.5 0.2 copy-done.6
  36.7 9.0 %fusion.28 = f32[1024,3,4,128]{0,3,2,1:T(8,128)S(1)} fusion(bf16[1,2048,3,4,128]{1,4,3,2,0:T(8,128)(2,1)} %copy.141, bf16[1024,2048]{1,0:T(8,128)(2,1)S(1)} %copy-done.6, f32[2048]{0:T(1024)S(1)} %bitcast.227, f32[1024]{0:T(1024)S(1)} %add_rsqrt_fusion.1), kind=kOutput, calls=%fused_computation.40 | convolution fusion | flops 6450839552 | bytes 16789504 | tf_op jit(solution)/shard_map/dot_general | solution.py:397
  45.8 1.0 multiply_cosine_fusion
  46.9 0.3 slice_bitcast_fusion.7
  47.3 1.1 copy-done.4
  48.5 0.7 subtract_convert_fusion.3
  49.2 0.2 pad_maximum_fusion.2
  49.4 1.6 copy.108
  51.0 6.4 all-to-all-start.1
  58.0 0.4 fusion.44
  58.4 10.2 %fusion.173 = (f32[4,1024]{1,0:T(4,128)S(1)}, f32[4,1024,1024]{1,2,0:T(8,128)}) fusion(pred[1024,1024]{0,1:T(8,128)(4,1)S(1)} %fusion.44, bf16[1024,4,64]{0,2,1:T(8,128)(2,1)S(1)} %get-tuple-element.82, bf16[1024,4,64]{0,2,1:T(8,128)(2,1)S(1)} %get-tuple-element.83, bf16[1024,4,64]{0,2,1:T(8,128)(2,1)S(1)} %get-tuple-element.75, ...), kind=kOutput, calls=%fused_computation.264 | convolution fusion | flops 1094714368 | bytes 19939328 | tf_op jit(solution)/shard_map/sub | solution.py:358
  68.6 3.1 fusion.171
  71.7 0.2 all-gather.10.cloned.1.call-start
  72.0 7.7 %fusion.67 = bf16[4,128,1024]{2,1,0:T(8,128)(2,1)S(1)} fusion(f32[4,1024,1024]{1,2,0:T(8,128)} %get-tuple-element.121, f32[4,1024]{1,0:T(4,128)S(1)} %get-tuple-element.120, f32[1024,3,4,128]{0,3,2,1:T(8,128)} %copy-done.4), kind=kOutput, calls=%fused_computation.93 | convolution fusion | flops 1082654720 | bytes 18890752 | tf_op jit(solution)/shard_map/hqk,khe->qhe/dot_general | solution.py:359
  79.7 1.3 copy.142.refs_0_
  81.3 0.6 fusion.172
  81.9 10.1 %fusion.169 = (bf16[1,2048,3,4,1,128]{5,3,4,2,1,0:T(4,128)(2,1)}, bf16[1,2048,3,4,1,128]{5,3,4,2,1,0:T(4,128)(2,1)S(1)}) fusion(bf16[2,2048,3,4,1,128]{5,3,4,2,1,0:T(4,128)(2,1)} %param.27), kind=kLoop, calls=%fused_computation.260 | loop fusion | bytes 25165824 | tf_op jit(solution)/shard_map/slice | solution.py:404
  92.0 1.0 fusion.25
  93.4 0.7 iota_compare_fusion.1
  94.0 0.2 copy-done.2
  94.3 2.4 slice_bitcast_fusion.9
  96.7 0.7 fusion.60
  97.8 2.5 slice_bitcast_fusion.8
  100.2 0.4 fusion.58
  100.7 1.0 convolution_bitcast_fusion.1.refs_1_
  101.7 80.4 %ctx_gather.2 = (bf16[4,1024,512]{2,1,0:T(8,128)(2,1)}, bf16[8,2048]{1,0:T(8,128)(2,1)}) custom-call(bf16[1024,512]{1,0:T(8,128)(2,1)} %copy.142.refs_0_, f32[8,2048]{1,0:T(8,128)} %convolution_bitcast_fusion.1.refs_1_), custom_call_target="tpu_custom_call" | custom-call | flops 70000001024 | bytes 5242880 | tf_op jit(solution)/shard_map/ctx_gather/pallas_call | solution.py:109
  182.1 10.6 %copy.144 = bf16[1,2048,3,4,128]{1,4,3,2,0:T(8,128)(2,1)} copy(bf16[1,2048,3,4,128]{4,3,2,1,0:T(4,128)(2,1)} %get-tuple-element.59) | data formatting | bytes 12582912 | tf_op jit(solution)/shard_map/squeeze | solution.py:397
  192.9 5.8 fusion.45
  198.8 4.1 fusion.32.refs_6_
  202.9 1.6 collective-permute-start.1
  204.5 181.4 %mlp_sum.2 = (bf16[1024,2048]{1,0:T(8,128)(2,1)}, bf16[8,2048]{1,0:T(8,128)(2,1)}) custom-call(bf16[4,1024,512]{2,1,0:T(8,128)(2,1)} %get-tuple-element.18.refs_0_, bf16[1024,2048]{1,0:T(8,128)(2,1)} %refs_1_.1, bf16[8,4,64,2048]{3,2,1,0:T(8,128)(2,1)} %bitcast.229, bf16[2,2,1376,2048]{3,2,1,0:T(8,128)(2,1)} %refs_3_.3, bf16[2,1376,2048]{2,1,0:T(8,128)(2,1)} %refs_4_.3, ...), custom_call_target="tpu_custom_call" | custom-call | flops 160000000000 | bytes 41943040 | tf_op jit(solution)/shard_map/mlp_sum/pallas_call | solution.py:296
  385.9 3.2 fusion.13
  389.2 0.2 copy-done.9
  389.4 9.2 %fusion.26 = f32[1024,3,4,128]{0,3,2,1:T(8,128)S(1)} fusion(bf16[1,2048,3,4,128]{1,4,3,2,0:T(8,128)(2,1)} %copy.144, bf16[1024,2048]{1,0:T(8,128)(2,1)S(1)} %copy-done.9, f32[2048]{0:T(1024)S(1)} %bitcast.226, f32[1024]{0:T(1024)S(1)} %add_rsqrt_fusion), kind=kOutput, calls=%fused_computation.38 | convolution fusion | flops 6450839552 | bytes 16789504 | tf_op jit(solution)/shard_map/dot_general | solution.py:397
  398.7 0.3 slice_bitcast_fusion.3
  399.0 2.4 copy-done.5
  401.5 0.7 subtract_convert_fusion.1
  402.3 1.6 pad_maximum_fusion.1
  403.8 0.5 collective-permute-start
  404.4 10.1 %fusion.174 = (f32[4,1024]{1,0:T(4,128)S(1)}, f32[4,1024,1024]{1,2,0:T(8,128)}) fusion(pred[1024,1024]{0,1:T(8,128)(4,1)S(1)} %copy-done.16, bf16[1024,4,64]{0,2,1:T(8,128)(2,1)S(1)} %get-tuple-element.80, bf16[1024,4,64]{0,2,1:T(8,128)(2,1)S(1)} %get-tuple-element.81, bf16[1024,4,64]{0,2,1:T(8,128)(2,1)S(1)} %get-tuple-element.71, ...), kind=kOutput, calls=%fused_computation.265 | convolution fusion | flops 1094714368 | bytes 19939328 | tf_op jit(solution)/shard_map/sub | solution.py:358
  414.5 7.7 %fusion.66 = bf16[4,128,1024]{2,1,0:T(8,128)(2,1)S(1)} fusion(f32[4,1024,1024]{1,2,0:T(8,128)} %get-tuple-element.123, f32[4,1024]{1,0:T(4,128)S(1)} %get-tuple-element.122, f32[1024,3,4,128]{0,3,2,1:T(8,128)} %copy-done.5), kind=kOutput, calls=%fused_computation.92 | convolution fusion | flops 1082654720 | bytes 18890752 | tf_op jit(solution)/shard_map/hqk,khe->qhe/dot_general | solution.py:359
  422.3 1.3 copy.145.refs_0_
  423.8 3.9 fusion.24
  428.1 0.6 fusion.56
  429.1 0.4 fusion.54
  429.5 1.1 convolution_bitcast_fusion.refs_1_
  430.6 71.5 %ctx_gather.3 = (bf16[4,1024,512]{2,1,0:T(8,128)(2,1)}, bf16[8,2048]{1,0:T(8,128)(2,1)}) custom-call(bf16[1024,512]{1,0:T(8,128)(2,1)} %copy.145.refs_0_, f32[8,2048]{1,0:T(8,128)} %convolution_bitcast_fusion.refs_1_), custom_call_target="tpu_custom_call" | custom-call | flops 70000001024 | bytes 5242880 | tf_op jit(solution)/shard_map/ctx_gather/pallas_call | solution.py:109
  502.2 0.7 fusion.144
  503.0 7.5 %broadcast_select_fusion = (bf16[2,8,256,4,1,128]{5,3,4,2,1,0:T(4,128)(2,1)}, bf16[2,8,256,4,1,128]{5,3,4,2,1,0:T(4,128)(2,1)}) fusion(bf16[2,8,256,4,1,128]{5,3,4,2,1,0:T(4,128)(2,1)S(1)} %copy-done.1, pred[8,256]{1,0:T(8,128)(4,1)S(1)} %copy-done.40, bf16[2,8,4,128]{3,2,1,0:T(4,128)(2,1)S(1)} %copy.110, bf16[2,8,256,4,1,128]{5,3,4,2,1,0:T(4,128)(2,1)} %param.24, ...), kind=kLoop, calls=%fused_computation.58 | loop fusion | flops 4194304 | bytes 16812032 | tf_op jit(solution)/shard_map/jit(_where)/select_n | solution.py:430
  510.5 3.1 copy.107
  513.6 4.5 all-to-all-start
  518.2 5.8 fusion.48
  524.1 4.1 fusion.30.refs_6_
  528.2 185.6 %mlp_sum.3 = (bf16[1024,2048]{1,0:T(8,128)(2,1)}, bf16[8,2048]{1,0:T(8,128)(2,1)}) custom-call(bf16[4,1024,512]{2,1,0:T(8,128)(2,1)} %get-tuple-element.22.refs_0_, bf16[1024,2048]{1,0:T(8,128)(2,1)} %get-tuple-element.20.refs_1_, bf16[8,4,64,2048]{3,2,1,0:T(8,128)(2,1)} %bitcast.228, bf16[2,2,1376,2048]{3,2,1,0:T(8,128)(2,1)} %refs_3_.3, ...), custom_call_target="tpu_custom_call" | custom-call | flops 160000000000 | bytes 41943040 | tf_op jit(solution)/shard_map/mlp_sum/pallas_call | solution.py:296
  713.8 1.4 fusion.89
  715.2 3.3 fusion.53
  718.6 4.2 copy.111
  722.8 2.5 copy.112
  725.3 4.8 copy.194
  (132 shorter events, 3.0 us)
Async XLA Ops:
  7.2 61.4 %all-gather.6.cloned.1.call-start = ((), (), s32[]{:S(2)}) async-start(), calls=%async_computation.2 | async-start | bytes 2621440 | tf_op jit(solution)/shard_map/all_gather | solution.py:440
  33.2 3.4 copy-start.6
  45.7 2.6 copy-start.4
  46.8 1.7 copy-start.10
  46.8 1.7 copy-start.12
  49.4 8.0 %copy-start.42 = (s32[8]{0:T(128)S(1)}, s32[8]{0:T(128)}, u32[]{:S(2)}) copy-start(s32[8]{0:T(128)} %param.26) | copy-start | bytes 100
  51.0 151.9 %all-to-all-start.1 = ((bf16[2,1024,4,128]{1,3,0,2:T(8,128)(2,1)}), bf16[2,1024,4,128]{1,3,0,2:T(8,128)(2,1)}, u32[]{:S(2)}, u32[]{:S(2)}) async-start(bf16[2,1024,4,128]{1,3,0,2:T(8,128)(2,1)} %copy.108), calls=%async_computation.1 | async-start | bytes 4194304 | tf_op jit(solution)/shard_map/all_to_all | solution.py:416
  57.4 147.1 %all-gather.8.cloned.1.call-start = ((), (), s32[]{:S(2)}) async-start(), calls=%async_computation.3 | async-start | bytes 9437184 | tf_op jit(solution)/shard_map/all_gather | solution.py:441
  58.4 10.2 %copy-start.15 = (pred[1024,1024]{0,1:T(8,128)(4,1)}, pred[1024,1024]{0,1:T(8,128)(4,1)S(1)}, u32[]{:S(2)}) copy-start(pred[1024,1024]{0,1:T(8,128)(4,1)S(1)} %fusion.44) | copy-start | bytes 3145732
  71.7 456.4 %all-gather.10.cloned.1.call-start = ((), (), s32[]{:S(2)}) async-start(), calls=%async_computation.4 | async-start | bytes 9437184 | tf_op jit(solution)/shard_map/all_gather | solution.py:441
  72.0 9.1 %copy-start.17 = (bf16[8,2048]{1,0:T(8,128)(2,1)S(1)}, bf16[8,2048]{1,0:T(8,128)(2,1)}, u32[]{:S(2)}) copy-start(bf16[8,2048]{1,0:T(8,128)(2,1)} %param.23) | copy-start | bytes 98308
  72.0 9.3 %copy-start.37 = (f32[2,2,2048]{2,1,0:T(2,128)S(1)}, f32[2,2,2048]{2,1,0:T(2,128)}, u32[]{:S(2)}) copy-start(f32[2,2,2048]{2,1,0:T(2,128)} %param.31) | copy-start | bytes 98308
  81.3 11.7 %copy-start.32 = (f32[8,64]{1,0:T(8,128)}, f32[8,64]{1,0:T(8,128)S(1)}, u32[]{:S(2)}) copy-start(f32[8,64]{1,0:T(8,128)S(1)} %get-tuple-element.116) | copy-start | bytes 6148
  81.3 11.7 %copy-start.34 = (f32[8,64]{1,0:T(8,128)}, f32[8,64]{1,0:T(8,128)S(1)}, u32[]{:S(2)}) copy-start(f32[8,64]{1,0:T(8,128)S(1)} %get-tuple-element.117) | copy-start | bytes 6148
  92.0 2.2 copy-start.2
  93.0 7.6 %copy-start.25 = (f32[8,3,4,128]{3,0,2,1:T(8,128)}, f32[8,3,4,128]{3,0,2,1:T(8,128)S(1)}, u32[]{:S(2)}) copy-start(f32[8,3,4,128]{3,0,2,1:T(8,128)S(1)} %fusion.25) | copy-start | bytes 147460
  93.1 3.6 copy-start.28
  93.1 3.6 copy-start.30
  94.3 3.4 copy-start.26
  94.3 3.5 copy-start
  97.7 2.9 copy-start.7
  182.1 10.7 %copy-start.21 = (bf16[8,2048]{1,0:T(8,128)(2,1)S(1)}, bf16[8,2048]{1,0:T(8,128)(2,1)}, u32[]{:S(2)}) copy-start(bf16[8,2048]{1,0:T(8,128)(2,1)} %get-tuple-element.19) | copy-start | bytes 98308
  202.9 512.3 %collective-permute-start.1 = (bf16[2,1024,4,128]{1,3,0,2:T(8,128)(2,1)}, bf16[2,1024,4,128]{1,3,0,2:T(8,128)(2,1)}, u32[]{:S(2)}, u32[]{:S(2)}) collective-permute-start(bf16[2,1024,4,128]{1,3,0,2:T(8,128)(2,1)} %all-to-all-done.1), channel_id=1, source_target_pairs={{0,2},{1,3},{2,0},{3,1},{4,6},{5,7},{6,4},{7,5},{8,10},{9,11},{10,... | collective-permute-start | bytes 6291464 | tf_op jit(solution)/shard_map/ppermute | solution.py:417
  385.9 3.5 copy-start.9
  385.9 3.4 copy-start.41
  398.6 2.7 copy-start.5
  398.6 2.9 copy-start.11
  398.6 2.9 copy-start.13
  401.5 2.8 copy-start.16
  403.8 106.6 %collective-permute-start = (bf16[2,1024,4,128]{1,3,2,0:T(8,128)(2,1)}, bf16[2,1024,4,128]{1,3,2,0:T(8,128)(2,1)}, u32[]{:S(2)}, u32[]{:S(2)}) collective-permute-start(bf16[2,1024,4,128]{1,3,2,0:T(8,128)(2,1)} %pad_maximum_fusion.1), channel_id=1, source_target_pairs={{0,2},{1,3},{2,0},{3,1},{4,6},{5,7},{6,4},{7,5},{8,10},{9,11},{10,... | collective-permute-start | bytes 6291464 | tf_op jit(solution)/shard_map/ppermute | solution.py:419
  414.5 9.1 %copy-start.18 = (bf16[8,2048]{1,0:T(8,128)(2,1)S(1)}, bf16[8,2048]{1,0:T(8,128)(2,1)}, u32[]{:S(2)}) copy-start(bf16[8,2048]{1,0:T(8,128)(2,1)} %param.23) | copy-start | bytes 98308
  414.5 9.1 %copy-start.22 = (bf16[8,2048]{1,0:T(8,128)(2,1)S(1)}, bf16[8,2048]{1,0:T(8,128)(2,1)}, u32[]{:S(2)}) copy-start(bf16[8,2048]{1,0:T(8,128)(2,1)} %get-tuple-element.19) | copy-start | bytes 98308
  414.5 9.1 %copy-start.38 = (bf16[8,2048]{1,0:T(8,128)(2,1)S(1)}, bf16[8,2048]{1,0:T(8,128)(2,1)}, u32[]{:S(2)}) copy-start(bf16[8,2048]{1,0:T(8,128)(2,1)} %get-tuple-element.21) | copy-start | bytes 98308
  414.5 9.3 %copy-start.36 = (f32[1,1,2048]{2,1,0:T(1,128)S(1)}, f32[1,1,2048]{2,1,0:T(1,128)}, u32[]{:S(2)}) copy-start(f32[1,1,2048]{2,1,0:T(1,128)} %get-tuple-element.91) | copy-start | bytes 24580
  422.2 5.5 copy-start.33
  422.3 5.5 copy-start.35
  422.3 5.8 copy-start.3
  423.7 94.5 %copy-start.19 = (bf16[8,2048]{1,0:T(8,128)(2,1)}, bf16[8,2048]{1,0:T(8,128)(2,1)S(1)}, u32[]{:S(2)}) copy-start(bf16[8,2048]{1,0:T(8,128)(2,1)S(1)} %get-tuple-element.55) | copy-start | bytes 98308
  423.8 4.9 copy-start.27
  423.8 5.3 copy-start.14
  423.8 5.7 copy-start.8
  430.6 71.5 %copy-start.29 = (bf16[8,4,64]{2,0,1:T(8,128)(2,1)S(1)}, bf16[8,4,64]{2,0,1:T(8,128)(2,1)}, u32[]{:S(2)}) copy-start(bf16[8,4,64]{2,0,1:T(8,128)(2,1)} %copy-done.28) | copy-start | bytes 12292
  430.6 71.5 %copy-start.31 = (bf16[8,4,64]{2,0,1:T(8,128)(2,1)S(1)}, bf16[8,4,64]{2,0,1:T(8,128)(2,1)}, u32[]{:S(2)}) copy-start(bf16[8,4,64]{2,0,1:T(8,128)(2,1)} %copy-done.30) | copy-start | bytes 12292
  430.6 72.4 %copy-start.1 = (bf16[2,8,256,4,1,128]{5,3,4,2,1,0:T(4,128)(2,1)S(1)}, bf16[2,8,256,4,1,128]{5,3,4,2,1,0:T(4,128)(2,1)}, u32[]{:S(2)}) copy-start(bf16[2,8,256,4,1,128]{5,3,4,2,1,0:T(4,128)(2,1)} %param.25) | copy-start | bytes 12582916
  430.6 72.4 %copy-start.40 = (pred[8,256]{1,0:T(8,128)(4,1)S(1)}, pred[8,256]{1,0:T(8,128)(4,1)}, u32[]{:S(2)}) copy-start(pred[8,256]{1,0:T(8,128)(4,1)} %get-tuple-element.118) | copy-start | bytes 6148
  510.5 7.6 %copy-start.23 = (bf16[8,2048]{1,0:T(8,128)(2,1)S(1)}, bf16[8,2048]{1,0:T(8,128)(2,1)}, u32[]{:S(2)}) copy-start(bf16[8,2048]{1,0:T(8,128)(2,1)} %get-tuple-element.24) | copy-start | bytes 98308
  510.5 7.8 %copy-start.39 = (f32[1,1,2048]{2,1,0:T(1,128)S(1)}, f32[1,1,2048]{2,1,0:T(1,128)}, u32[]{:S(2)}) copy-start(f32[1,1,2048]{2,1,0:T(1,128)} %get-tuple-element.88) | copy-start | bytes 24580
  513.6 201.7 %all-to-all-start = ((bf16[2,1024,4,128]{1,3,0,2:T(8,128)(2,1)}), bf16[2,1024,4,128]{1,3,0,2:T(8,128)(2,1)}, u32[]{:S(2)}, u32[]{:S(2)}) async-start(bf16[2,1024,4,128]{1,3,0,2:T(8,128)(2,1)} %copy.107), calls=%async_computation | async-start | bytes 4194304 | tf_op jit(solution)/shard_map/all_to_all | solution.py:421
  528.2 185.6 %copy-start.20 = (bf16[8,2048]{1,0:T(8,128)(2,1)S(1)}, bf16[8,2048]{1,0:T(8,128)(2,1)}, u32[]{:S(2)}) copy-start(bf16[8,2048]{1,0:T(8,128)(2,1)} %copy-done.19) | copy-start | bytes 98308
  528.2 185.6 %copy-start.24 = (bf16[8,2048]{1,0:T(8,128)(2,1)S(1)}, bf16[8,2048]{1,0:T(8,128)(2,1)}, u32[]{:S(2)}) copy-start(bf16[8,2048]{1,0:T(8,128)(2,1)} %get-tuple-element.24) | copy-start | bytes 98308
Sparse Core Ops, SparseCore 0:
  10.1 48.0 all-gather.5
  71.9 55.4 all-gather.7
  203.0 81.3 all-gather.9
